TPU v7x, 32 devices: a whole 2x2x4 slice. The times are simulated.
32 devices in a mesh: gx: 4 (over x, core), gy: 8 (over z, y).
Axes of the slice: x: 2, y: 2, z: 4, core: 2. Of those that a mesh axis runs over, the one named last changes fastest.
Arguments:
- substrate: float32 [16, 64, 1024], P(None, 'gy', 'gx'), may hold values from 0 to 1
- catalyst: float32 [16, 64, 1024], P(None, 'gy', 'gx'), may hold values from 0 to 1
Outputs:
- substrate_next: float32 [16, 64, 1024], P(None, 'gy', 'gx')
- catalyst_next: float32 [16, 64, 1024], P(None, 'gy', 'gx')
- rebuilt: float32 [2, 16, 1024, 64], P(None, None, ('gx', 'gy'))
All inputs are finite; a program needn't handle non-finite values.
Results may differ from a plain program's by a relative error of at most 0.00002.
Values sent between devices are 32-bit elements; how exact they have to be, the bound alone decides.
A program may use at most 64 MiB of HBM per device.

v0:
```python
import functools

import jax
import jax.numpy as jnp
from jax import lax
from jax.experimental import pallas as pl
from jax.experimental.pallas import tpu as pltpu
from jax.sharding import PartitionSpec as P

feed_rate = 0.037
kill_rate = 0.06
substrate_diffusion = 0.15
catalyst_diffusion = 0.08

MESH = pl.DeviceIdType.MESH
LANES = 128


def react(substrate, catalyst, spread_substrate, spread_catalyst):
    reaction = substrate * catalyst * catalyst
    new_substrate = (
        substrate
        + substrate_diffusion * spread_substrate
        - reaction
        + feed_rate * (1.0 - substrate)
    )
    new_catalyst = (
        catalyst
        + catalyst_diffusion * spread_catalyst
        + reaction
        - (feed_rate + kill_rate) * catalyst
    )
    return new_substrate, new_catalyst


def split(value):
    high = value.astype(jnp.bfloat16)
    low = (value - high.astype(jnp.float32)).astype(jnp.bfloat16)
    return high, low


def spread_of(before, here, after):
    planes, extent = here.shape
    total = pltpu.roll(here, 1, 0) + pltpu.roll(here, planes - 1, 0)
    total = total + before + after
    total = total + pltpu.roll(here, 1, 1) + pltpu.roll(here, extent - 1, 1)
    return total - 6.0 * here


def partner_of(me, step, size):
    if size & (size - 1):
        return lax.rem(me + step, size)
    partner = me + step
    for bit in range(size.bit_length() - 1):
        if step >> bit & 1:
            partner = partner - 2 * (1 << bit) * lax.rem(me // (1 << bit), 2)
    return partner


def kernel(dims, *refs):
    planes, columns, extent, owners, slabs_x, slabs_y = dims
    (u_ref, v_ref, u_out, v_out, gathered, loaded, state, edge, packed, got, relay, relayed, middle, sums,
     outgoing, load_sem, send_sem, recv_sem, deal_send, deal_recv) = refs
    tiles = extent // LANES
    gx, gy = lax.axis_index("gx"), lax.axis_index("gy")

    barrier = pltpu.get_barrier_semaphore()
    sides = [(lax.rem(gx + shift, slabs_x), gy) for shift in (1, slabs_x - 1)]
    ends = [(gx, lax.rem(gy + shift, owners)) for shift in (1, owners - 1)]
    peers = [(gx, lax.rem(gy + step, owners)) for step in range(1, owners)]
    for device in sides + peers:
        pl.semaphore_signal(barrier, inc=1, device_id=device, device_id_type=MESH)

    loads = [
        pltpu.make_async_copy(source, loaded.at[field], load_sem.at[field])
        for field, source in enumerate((u_ref, v_ref))
    ]
    for load in loads:
        load.start()
    for load in loads:
        load.wait()

    lane = lax.broadcasted_iota(jnp.int32, (planes, LANES), 1)
    group = lax.rem(lane + 2, LANES) // 4
    pack = jnp.zeros((planes, LANES), jnp.float32)
    for field in range(2):
        for column in range(columns):
            slab = jnp.concatenate(
                [
                    loaded[field, pl.ds(tile * columns + column, planes, stride=tiles * columns), :]
                    for tile in range(tiles)
                ],
                axis=1,
            )
            state[field, 2 + column] = slab
            at = field * columns + column
            tips = jnp.where(lane < LANES // 2, slab[:, :LANES], slab[:, extent - LANES :])
            tips = pltpu.roll(tips, 4 * at, 1) if at else tips
            pack = jnp.where(group == at, tips, pack)
    packed[...] = pack

    pl.semaphore_wait(barrier, len(sides) + len(peers))

    def send(number, source, target, device):
        return pltpu.make_async_remote_copy(
            src_ref=source,
            dst_ref=target,
            send_sem=send_sem.at[number],
            recv_sem=recv_sem.at[number],
            device_id=device,
            device_id_type=MESH,
        )

    low_end, high_end = slice(0, 2), slice(columns + 2, columns + 4)
    across = [send(2 + side, packed, got.at[side], sides[side]) for side in range(2)]
    along = [
        send(0, state.at[:, columns : columns + 2], state.at[:, low_end], ends[0]),
        send(1, state.at[:, 2:4], state.at[:, high_end], ends[1]),
    ]
    corners = [send(4 + side, relay, relayed.at[side], ends[side]) for side in range(2)]
    for copy in across + along:
        copy.start()

    half = extent // 2
    row = lax.broadcasted_iota(jnp.int32, (half, extent), 0)
    fine = lax.broadcasted_iota(jnp.int32, (half, extent), 1)
    to_blend = jnp.concatenate(
        [
            jnp.where(fine // 2 == row, 0.125, 0.0),
            jnp.where(fine // 4 == row // 2, 0.03125, 0.0),
        ],
        axis=1,
    ).astype(jnp.bfloat16)

    for copy in across:
        copy.wait_recv()

    both = jnp.where(lax.rem(lane, 4) < 2, got[1], got[0])
    relay[...] = both

    def place(field, c, tile, column):
        at = field * columns + column
        edge[field, c] = pltpu.roll(tile, LANES - 4 * at, 1) if at else tile

    for field in range(2):
        for c in range(2, columns + 2):
            place(field, c, both, c - 2)
    for copy in corners:
        copy.start()

    def wide(field, c):
        if c in (0, columns + 3):
            tail = jnp.zeros((planes, LANES), jnp.float32)
        else:
            tail = edge[field, c]
        return jnp.concatenate([state[field, c], tail], axis=1)

    def first(c):
        u, v = wide(0, c), wide(1, c)
        su = spread_of(wide(0, c - 1), u, wide(0, c + 1))
        sv = spread_of(wide(1, c - 1), v, wide(1, c + 1))
        middle[0, c], middle[1, c] = react(u, v, su, sv)

    level = [{}, {}]

    def second(c):
        u, v = middle[0, c], middle[1, c]
        su = spread_of(middle[0, c - 1], u, middle[0, c + 1])
        sv = spread_of(middle[1, c - 1], v, middle[1, c + 1])
        new = react(u[:, :extent], v[:, :extent], su[:, :extent], sv[:, :extent])
        for field, out in enumerate((u_out, v_out)):
            for tile in range(tiles):
                rows = pl.ds(tile * columns + c - 2, planes, stride=tiles * columns)
                out[rows, :] = new[field][:, tile * LANES : (tile + 1) * LANES]
            level[field][c - 2] = new[field]

    for c in range(3, columns + 1):
        first(c)
    for c in range(4, columns):
        second(c)
    for side, (outer, steps, last) in enumerate(
        ((1, (1, 2), (2, 3)), (columns + 2, (columns + 2, columns + 1), (columns + 1, columns)))
    ):
        along[side].wait_recv()
        corners[side].wait_recv()
        for field in range(2):
            place(field, outer, relayed[side], (1 - side) * (columns - 1))
        for c in steps:
            first(c)
        for c in last:
            second(c)

    pairs = columns // 2
    for field in range(2):
        twos = [level[field][2 * k] + level[field][2 * k + 1] for k in range(pairs)]
        fours = [twos[2 * q] + twos[2 * q + 1] for q in range(pairs // 2)]
        for k in range(pairs):
            rows = pl.ds(field * planes * pairs + k, planes, stride=pairs)
            for tile in range(tiles):
                lanes = slice(tile * LANES, (tile + 1) * LANES)
                sums[tile, rows, :] = twos[k][:, lanes]
                sums[tiles + tile, rows, :] = fours[k // 2][:, lanes]

    contract = (((1,), (1,)), ((), ()))
    high, low = split(jnp.concatenate([sums[tile] for tile in range(2 * tiles)], axis=1))
    blend = lax.dot_general(to_blend, high, contract, preferred_element_type=jnp.float32)
    blend += lax.dot_general(to_blend, low, contract, preferred_element_type=jnp.float32)
    portion = half // owners
    for owner in range(owners):
        outgoing[owner] = blend[owner * portion : (owner + 1) * portion]

    deals = []
    for step in range(owners - 1, 0, -1):
        partner = partner_of(gy, step, owners)
        deals.append(
            pltpu.make_async_remote_copy(
                src_ref=outgoing.at[partner],
                dst_ref=gathered.at[gy],
                send_sem=deal_send.at[step - 1],
                recv_sem=deal_recv.at[step - 1],
                device_id=(gx, partner),
                device_id_type=MESH,
            )
        )
        deals[-1].start()
    gathered[gy] = outgoing[gy]

    for deal in deals:
        deal.wait_recv()

    for copy in across + along + corners:
        copy.wait_send()
    for deal in deals:
        deal.wait_send()


def finish(u_ref, v_ref, dealt, u_out, v_out, rebuilt_out, doubled, rebuilt, sems):
    copies = [
        pltpu.make_async_copy(u_ref, u_out, sems.at[0]),
        pltpu.make_async_copy(v_ref, v_out, sems.at[1]),
    ]
    for copy in copies:
        copy.start()

    owners, portion, _ = dealt.shape
    wide_in = lax.broadcasted_iota(jnp.int32, (LANES, 4 * LANES), 0)
    wide_out = lax.broadcasted_iota(jnp.int32, (LANES, 4 * LANES), 1)
    column_of = wide_in // 16 * 4 + wide_in % 4
    spreading = jnp.where(
        (wide_in // 4 % 4 == wide_out // LANES) & (column_of == wide_out % LANES // 2),
        1.0,
        0.0,
    ).astype(jnp.bfloat16)
    lane = lax.broadcasted_iota(jnp.int32, (portion, LANES), 1)
    blocks = [dealt[owner] for owner in range(owners)]
    width, rows = rebuilt.shape[1], 2 * portion
    chunks = 4
    share = 8 // chunks
    for chunk in range(chunks):
        for h in range(chunk * share, (chunk + 1) * share):
            part = jnp.zeros((portion, LANES), jnp.float32)
            for owner in range(8):
                shift = (16 * (owner - h)) % LANES
                moved = pltpu.roll(blocks[owner], shift, 1) if shift else blocks[owner]
                part = jnp.where(lane // 16 == owner, moved, part)
            doubled[pl.ds(h * rows, portion, stride=2), :] = part
            doubled[pl.ds(h * rows + 1, portion, stride=2), :] = part
        high, low = split(doubled[chunk * share * rows : (chunk + 1) * share * rows, :])
        whole = jnp.dot(high, spreading, preferred_element_type=jnp.float32)
        whole += jnp.dot(low, spreading, preferred_element_type=jnp.float32)
        for h in range(share):
            for z in range(4):
                base = ((chunk * share + h) * 4 + z) * rows
                rebuilt[base : base + rows, :] = whole[
                    h * rows : (h + 1) * rows, z * LANES : z * LANES + width
                ]
        size = share * 4 * rows
        copies.append(
            pltpu.make_async_copy(
                rebuilt.at[chunk * size : (chunk + 1) * size],
                rebuilt_out.at[chunk * size : (chunk + 1) * size],
                sems.at[2 + chunk],
            )
        )
        copies[-1].start()
    for copy in copies:
        copy.wait()


def tiled(field):
    planes, columns, extent = field.shape
    field = field.reshape(planes, columns, extent // LANES, LANES)
    return jnp.transpose(field, (0, 2, 1, 3)).reshape(-1, LANES)


def untiled(field, shape):
    planes, columns, extent = shape
    field = field.reshape(planes, extent // LANES, columns, LANES)
    return jnp.transpose(field, (0, 2, 1, 3)).reshape(shape)


def body(substrate, catalyst):
    planes, columns, extent = substrate.shape
    slabs_x, owners = lax.axis_size("gx"), lax.axis_size("gy")
    half, pairs, tiles = extent // 2, columns // 2, extent // LANES
    portion = half // owners
    values = 2 * planes * pairs
    fused = (
        planes == 16 and pairs == 4 and owners == 8 and values == LANES and portion % 8 == 0
    )
    dims = (planes, columns, extent, owners, slabs_x, owners)
    f32 = jnp.float32
    flat = (planes * tiles * columns, LANES)
    vmem = pl.BlockSpec(memory_space=pltpu.VMEM)
    anywhere = pl.BlockSpec(memory_space=pl.ANY)
    u, v, dealt = pl.pallas_call(
        functools.partial(kernel, dims),
        out_shape=(
            pltpu.VMEM(flat, f32),
            pltpu.VMEM(flat, f32),
            pltpu.VMEM((owners, portion, values), f32),
        ),
        in_specs=[anywhere] * 2,
        out_specs=(vmem,) * 3,
        scratch_shapes=[
            pltpu.VMEM((2,) + flat, f32),
            pltpu.VMEM((2, columns + 4, planes, extent), f32),
            pltpu.VMEM((2, columns + 4, planes, LANES), f32),
            pltpu.VMEM((planes, LANES), f32),
            pltpu.VMEM((2, planes, LANES), f32),
            pltpu.VMEM((planes, LANES), f32),
            pltpu.VMEM((2, planes, LANES), f32),
            pltpu.VMEM((2, columns + 4, planes, extent + LANES), f32),
            pltpu.VMEM((2 * tiles, values, LANES), f32),
            pltpu.VMEM((owners, portion, values), f32),
            pltpu.SemaphoreType.DMA((2,)),
            pltpu.SemaphoreType.DMA((6,)),
            pltpu.SemaphoreType.DMA((6,)),
            pltpu.SemaphoreType.DMA((owners - 1,)),
            pltpu.SemaphoreType.DMA((owners - 1,)),
        ],
        compiler_params=pltpu.CompilerParams(collective_id=0, has_side_effects=True),
    )(tiled(substrate), tiled(catalyst))
    rows, width = 2 * portion, columns * owners
    if fused:
        u, v, dealt = (
            pltpu.with_memory_space_constraint(x, pltpu.VMEM) for x in (u, v, dealt)
        )
        u, v, rebuilt = pl.pallas_call(
            finish,
            out_shape=(
                jax.ShapeDtypeStruct(flat, f32),
                jax.ShapeDtypeStruct(flat, f32),
                jax.ShapeDtypeStruct((2 * planes * rows, width), f32),
            ),
            in_specs=[vmem] * 3,
            out_specs=(anywhere,) * 3,
            scratch_shapes=[
                pltpu.VMEM((8 * rows, LANES), f32),
                pltpu.VMEM((2 * planes * rows, width), f32),
                pltpu.SemaphoreType.DMA((6,)),
            ],
        )(u, v, dealt)
        rebuilt = rebuilt.reshape(2, planes, rows, width)
    else:
        blend = dealt.reshape(owners, portion, 2, planes, pairs)
        blend = jnp.transpose(blend, (2, 3, 1, 0, 4)).reshape(2, planes, portion, owners * pairs)
        rebuilt = jnp.repeat(jnp.repeat(blend, 2, axis=2), 2, axis=3)
    return untiled(u, substrate.shape), untiled(v, substrate.shape), rebuilt


def solution(mesh):
    in_specs = (P(None, "gy", "gx"), P(None, "gy", "gx"))
    out_specs = (P(None, "gy", "gx"), P(None, "gy", "gx"), P(None, None, ("gx", "gy"), None))
    return jax.shard_map(body, mesh=mesh, in_specs=in_specs, out_specs=out_specs, check_vma=False)
```

profile of v0, /device:TPU:0, one launch (start us, length us, event | category | flops | bytes accessed | tf_op | source)
XLA Modules:
  0.0 18.6 jit_solution(24565508153213263)
XLA Ops:
  0.6 16.9 %shard_map.49 = (f32[256,128]{1,0:T(8,128)S(1)}, f32[256,128]{1,0:T(8,128)S(1)}, f32[8,16,128]{2,1,0:T(8,128)S(1)}) custom-call(f32[256,128]{1,0:T(8,128)} %bitcast.21, f32[256,128]{1,0:T(8,128)} %bitcast.22), custom_call_target="tpu_custom_call" | custom-call | tf_op jit(solution)/shard_map/pallas_call | solution.py:316
  17.5 1.1 %shard_map.50 = (f32[256,128]{1,0:T(8,128)}, f32[256,128]{1,0:T(8,128)}, f32[1024,64]{1,0:T(8,128)}) custom-call(f32[256,128]{1,0:T(8,128)S(1)} %get-tuple-element.9.u_ref, f32[256,128]{1,0:T(8,128)S(1)} %get-tuple-element.10.v_ref, f32[8,16,128]{2,1,0:T(8,128)S(1)} %get-tuple-element.11.dealt), custom_call_target="tpu_custom_call" | custom-call | tf_op jit(solution)/shard_map/pallas_call | solution.py:349
where the time goes:
time: 18.8 us; the launch traced here: 18.6 us
  Pallas kernels  18 us (96%)
  between operations  0.64 us (3%)
    pallas_call x1, Pallas kernels, body(): pl.pallas_call(functools.partial(kernel, dims), out_shape=(pltpu.VMEM(fla...  16.9 us
    pallas_call x1, Pallas kernels, body(): pl.pallas_call(finish, out_shape=(jax.ShapeDtypeStruct(flat, f32), jax.Sh...  1.11 us

commit v1 on v0

--- a/solution.py
+++ b/solution.py
@@ -59,7 +59,7 @@
 
 def kernel(dims, *refs):
     planes, columns, extent, owners, slabs_x, slabs_y = dims
-    (u_ref, v_ref, u_out, v_out, gathered, loaded, state, edge, packed, got, relay, relayed, middle, sums,
+    (u_ref, v_ref, u_out, v_out, gathered, loaded, state, edge, packed, got, corner, middle, sums,
      outgoing, load_sem, send_sem, recv_sem, deal_send, deal_recv) = refs
     tiles = extent // LANES
     gx, gy = lax.axis_index("gx"), lax.axis_index("gy")
@@ -68,7 +68,8 @@
     sides = [(lax.rem(gx + shift, slabs_x), gy) for shift in (1, slabs_x - 1)]
     ends = [(gx, lax.rem(gy + shift, owners)) for shift in (1, owners - 1)]
     peers = [(gx, lax.rem(gy + step, owners)) for step in range(1, owners)]
-    for device in sides + peers:
+    diagonals = [(side[0], end[1]) for end in ends for side in sides]
+    for device in sides + diagonals + peers:
         pl.semaphore_signal(barrier, inc=1, device_id=device, device_id_type=MESH)
 
     loads = [
@@ -99,7 +100,7 @@
             pack = jnp.where(group == at, tips, pack)
     packed[...] = pack
 
-    pl.semaphore_wait(barrier, len(sides) + len(peers))
+    pl.semaphore_wait(barrier, len(sides) + len(diagonals) + len(peers))
 
     def send(number, source, target, device):
         return pltpu.make_async_remote_copy(
@@ -117,8 +118,8 @@
         send(0, state.at[:, columns : columns + 2], state.at[:, low_end], ends[0]),
         send(1, state.at[:, 2:4], state.at[:, high_end], ends[1]),
     ]
-    corners = [send(4 + side, relay, relayed.at[side], ends[side]) for side in range(2)]
-    for copy in across + along:
+    corners = [send(4 + at, packed, corner.at[at], diagonals[at]) for at in range(4)]
+    for copy in across + corners + along:
         copy.start()
 
     half = extent // 2
@@ -135,8 +136,10 @@
     for copy in across:
         copy.wait_recv()
 
-    both = jnp.where(lax.rem(lane, 4) < 2, got[1], got[0])
-    relay[...] = both
+    def merged(ref, at):
+        return jnp.where(lax.rem(lane, 4) < 2, ref[at + 1], ref[at])
+
+    both = merged(got, 0)
 
     def place(field, c, tile, column):
         at = field * columns + column
@@ -145,9 +148,6 @@
     for field in range(2):
         for c in range(2, columns + 2):
             place(field, c, both, c - 2)
-    for copy in corners:
-        copy.start()
-
     def wide(field, c):
         if c in (0, columns + 3):
             tail = jnp.zeros((planes, LANES), jnp.float32)
@@ -182,9 +182,11 @@
         ((1, (1, 2), (2, 3)), (columns + 2, (columns + 2, columns + 1), (columns + 1, columns)))
     ):
         along[side].wait_recv()
-        corners[side].wait_recv()
+        for copy in corners[2 * side : 2 * side + 2]:
+            copy.wait_recv()
+        beyond = merged(corner, 2 * side)
         for field in range(2):
-            place(field, outer, relayed[side], (1 - side) * (columns - 1))
+            place(field, outer, beyond, (1 - side) * (columns - 1))
         for c in steps:
             first(c)
         for c in last:
@@ -328,14 +330,13 @@
             pltpu.VMEM((2, columns + 4, planes, LANES), f32),
             pltpu.VMEM((planes, LANES), f32),
             pltpu.VMEM((2, planes, LANES), f32),
-            pltpu.VMEM((planes, LANES), f32),
-            pltpu.VMEM((2, planes, LANES), f32),
+            pltpu.VMEM((4, planes, LANES), f32),
             pltpu.VMEM((2, columns + 4, planes, extent + LANES), f32),
             pltpu.VMEM((2 * tiles, values, LANES), f32),
             pltpu.VMEM((owners, portion, values), f32),
             pltpu.SemaphoreType.DMA((2,)),
-            pltpu.SemaphoreType.DMA((6,)),
-            pltpu.SemaphoreType.DMA((6,)),
+            pltpu.SemaphoreType.DMA((8,)),
+            pltpu.SemaphoreType.DMA((8,)),
             pltpu.SemaphoreType.DMA((owners - 1,)),
             pltpu.SemaphoreType.DMA((owners - 1,)),
         ],

time: 18.8 us -> 18.9 us (level)
  no operation moved by 1% of the time
where the time goes in v1:
time: 18.9 us; the launch traced here: 18.7 us
  Pallas kernels  18.1 us (96%)
  between operations  0.64 us (3%)
    pallas_call x1, Pallas kernels, body(): pl.pallas_call(functools.partial(kernel, dims), out_shape=(pltpu.VMEM(fla...  17 us
    pallas_call x1, Pallas kernels, body(): pl.pallas_call(finish, out_shape=(jax.ShapeDtypeStruct(flat, f32), jax.Sh...  1.11 us

profile of v1, /device:TPU:0, one launch (start us, length us, event | category | flops | bytes accessed | tf_op | source)
XLA Modules:
  0.0 18.7 jit_solution(10399180100404487675)
XLA Ops:
  0.6 17.0 %shard_map.49 = (f32[256,128]{1,0:T(8,128)S(1)}, f32[256,128]{1,0:T(8,128)S(1)}, f32[8,16,128]{2,1,0:T(8,128)S(1)}) custom-call(f32[256,128]{1,0:T(8,128)} %bitcast.21, f32[256,128]{1,0:T(8,128)} %bitcast.22), custom_call_target="tpu_custom_call" | custom-call | tf_op jit(solution)/shard_map/pallas_call | solution.py:318
  17.6 1.1 %shard_map.50 = (f32[256,128]{1,0:T(8,128)}, f32[256,128]{1,0:T(8,128)}, f32[1024,64]{1,0:T(8,128)}) custom-call(f32[256,128]{1,0:T(8,128)S(1)} %get-tuple-element.9.u_ref, f32[256,128]{1,0:T(8,128)S(1)} %get-tuple-element.10.v_ref, f32[8,16,128]{2,1,0:T(8,128)S(1)} %get-tuple-element.11.dealt), custom_call_target="tpu_custom_call" | custom-call | tf_op jit(solution)/shard_map/pallas_call | solution.py:350

commit v2 on v0

v2 whole, which is shorter than its diff:
```python
import functools

import jax
import jax.numpy as jnp
from jax import lax
from jax.experimental import pallas as pl
from jax.experimental.pallas import tpu as pltpu
from jax.sharding import PartitionSpec as P

feed_rate = 0.037
kill_rate = 0.06
substrate_diffusion = 0.15
catalyst_diffusion = 0.08

MESH = pl.DeviceIdType.MESH
LANES = 128


def react(substrate, catalyst, spread_substrate, spread_catalyst):
    reaction = substrate * catalyst * catalyst
    new_substrate = (
        substrate
        + substrate_diffusion * spread_substrate
        - reaction
        + feed_rate * (1.0 - substrate)
    )
    new_catalyst = (
        catalyst
        + catalyst_diffusion * spread_catalyst
        + reaction
        - (feed_rate + kill_rate) * catalyst
    )
    return new_substrate, new_catalyst


def split(value):
    high = value.astype(jnp.bfloat16)
    low = (value - high.astype(jnp.float32)).astype(jnp.bfloat16)
    return high, low


def spread_of(before, here, after):
    planes, extent = here.shape
    total = pltpu.roll(here, 1, 0) + pltpu.roll(here, planes - 1, 0)
    total = total + before + after
    total = total + pltpu.roll(here, 1, 1) + pltpu.roll(here, extent - 1, 1)
    return total - 6.0 * here


def partner_of(me, step, size):
    if size & (size - 1):
        return lax.rem(me + step, size)
    partner = me + step
    for bit in range(size.bit_length() - 1):
        if step >> bit & 1:
            partner = partner - 2 * (1 << bit) * lax.rem(me // (1 << bit), 2)
    return partner


def kernel(dims, *refs):
    planes, columns, extent, owners, slabs_x = dims
    (u_ref, v_ref, u_out, v_out, gathered, loaded, state, edge, packed, got, corner, middle, sums, outgoing,
     load_sem, send_sem, recv_sem, deal_send, deal_recv, late_send, late_recv, far) = refs
    tiles, pairs, last = extent // LANES, columns // 2, owners - 1
    gx, gy = lax.axis_index("gx"), lax.axis_index("gy")
    at_top, at_bottom = gy // last, (last - gy) // last

    barrier = pltpu.get_barrier_semaphore()
    across_of = [lax.rem(gx + shift, slabs_x) for shift in (1, slabs_x - 1)]
    along_of = [lax.rem(gy + shift, owners) for shift in (1, owners - 1)]

    def greet(semaphore, x, y):
        pl.semaphore_signal(semaphore, inc=1, device_id=(x, y), device_id_type=MESH)

    for x in across_of:
        greet(barrier, x, gy)
        greet(barrier, x, along_of[1])

    @pl.when(gy < last)
    def _():
        for x in across_of:
            greet(barrier, x, gy + 1)

    for peer in range(owners):

        @pl.when((peer > gy) | (peer == gy - 1))
        def _():
            greet(barrier, gx, peer)

    near_count = 4 + gy + (1 - at_top) + 2 * (1 - at_bottom)
    far_count = last - gy - 1 + 2 * at_bottom

    loads = [
        pltpu.make_async_copy(source, loaded.at[field], load_sem.at[field])
        for field, source in enumerate((u_ref, v_ref))
    ]
    for load in loads:
        load.start()
    for load in loads:
        load.wait()

    low = 4
    high = low + columns
    lane = lax.broadcasted_iota(jnp.int32, (planes, LANES), 1)
    group = lax.rem(lane + 2, LANES) // 4
    pack = jnp.zeros((planes, LANES), jnp.float32)
    for field in range(2):
        for column in range(columns):
            slab = jnp.concatenate(
                [
                    loaded[field, pl.ds(tile * columns + column, planes, stride=tiles * columns), :]
                    for tile in range(tiles)
                ],
                axis=1,
            )
            state[field, low + column] = slab
            at = field * columns + column
            tips = jnp.where(lane < LANES // 2, slab[:, :LANES], slab[:, extent - LANES :])
            tips = pltpu.roll(tips, 4 * at, 1) if at else tips
            pack = jnp.where(group == at, tips, pack)
    packed[...] = pack

    pl.semaphore_wait(barrier, near_count)

    def send(number, source, target, x, y):
        return pltpu.make_async_remote_copy(
            src_ref=source,
            dst_ref=target,
            send_sem=send_sem.at[number],
            recv_sem=recv_sem.at[number],
            device_id=(x, y),
            device_id_type=MESH,
        )

    up = send(0, state.at[:, high - 2 : high], state.at[:, low - 2 : low], gx, along_of[0])
    down = send(1, state.at[:, low : low + 2], state.at[:, high : high + 2], gx, along_of[1])
    wrap = send(2, state.at[:, high - 4 : high - 2], state.at[:, low - 4 : low - 2], gx, along_of[0])
    across = [send(3 + side, packed, got.at[side], across_of[side], gy) for side in range(2)]
    corners_up = [send(5 + side, packed, corner.at[0, side], across_of[side], along_of[0]) for side in range(2)]
    corners_down = [send(7 + side, packed, corner.at[1, side], across_of[side], along_of[1]) for side in range(2)]
    for copy in across + corners_up + [up]:
        copy.start()

    @pl.when(gy > 0)
    def _():
        for copy in corners_down + [down]:
            copy.start()

    @pl.when(gy == last)
    def _():
        wrap.start()
        for x in across_of:
            greet(far, x, 0)

    for peer in range(owners - 2):

        @pl.when(peer < gy - 1)
        def _():
            greet(far, gx, peer)

    half = extent // 2
    row = lax.broadcasted_iota(jnp.int32, (half, extent), 0)
    fine = lax.broadcasted_iota(jnp.int32, (half, extent), 1)
    to_level = jnp.where(fine // 2 == row, 0.25, 0.0).astype(jnp.bfloat16)

    for copy in across:
        copy.wait_recv()

    def merged(below, above):
        return jnp.where(lax.rem(lane, 4) < 2, above, below)

    def place(c, tips, column):
        for field in range(2):
            at = field * columns + column
            edge[field, c] = pltpu.roll(tips, LANES - 4 * at, 1) if at else tips

    both = merged(got[0], got[1])
    for column in range(columns):
        place(low + column, both, column)

    def wide(field, c, outer=()):
        tail = jnp.zeros((planes, LANES), jnp.float32) if c in outer else edge[field, c]
        return jnp.concatenate([state[field, c], tail], axis=1)

    def first(c, outer=()):
        u, v = wide(0, c), wide(1, c)
        su = spread_of(wide(0, c - 1, outer), u, wide(0, c + 1, outer))
        sv = spread_of(wide(1, c - 1, outer), v, wide(1, c + 1, outer))
        middle[0, c], middle[1, c] = react(u, v, su, sv)

    def second(c):
        u, v = middle[0, c], middle[1, c]
        su = spread_of(middle[0, c - 1], u, middle[0, c + 1])
        sv = spread_of(middle[1, c - 1], v, middle[1, c + 1])
        return react(u[:, :extent], v[:, :extent], su[:, :extent], sv[:, :extent])

    def pair(k, c, own=True):
        new = [second(c), second(c + 1)]
        for field, out in enumerate((u_out, v_out)):
            for tile in range(tiles):
                lanes = slice(tile * LANES, (tile + 1) * LANES)
                parts = [new[i][field][:, lanes] for i in range(2)]
                if own:
                    for i in range(2):
                        rows = pl.ds(tile * columns + c - low + i, planes, stride=tiles * columns)
                        out[rows, :] = parts[i]
                rows = pl.ds(field * planes * pairs + k, planes, stride=pairs)
                sums[tile, rows, :] = parts[0] + parts[1]

    def low_side(wrapped):
        up.wait_recv()
        for copy in corners_up:
            copy.wait_recv()
        beyond = merged(corner[0, 0], corner[0, 1])
        for step in range(1, 4 if wrapped else 2):
            place(low - step, beyond, columns - step)
        first(low)
        first(low - 1, () if wrapped else (low - 2,))
        pair(0, low)

    def high_side():
        down.wait_recv()
        for copy in corners_down:
            copy.wait_recv()
        place(high, merged(corner[1, 0], corner[1, 1]), 0)
        first(high - 1)
        first(high, (high + 1,))
        pair(pairs - 1, high - 2)

    def level_of():
        contract = (((1,), (1,)), ((), ()))
        upper, lower = split(jnp.concatenate([sums[tile] for tile in range(tiles)], axis=1))
        level = lax.dot_general(to_level, upper, contract, preferred_element_type=jnp.float32)
        return level + lax.dot_general(to_level, lower, contract, preferred_element_type=jnp.float32)

    portion = half // owners

    for c in range(low + 1, high - 1):
        first(c)
    for k in range(1, pairs - 1):
        pair(k, low + 2 * k)

    @pl.when(gy > 0)
    def _():
        low_side(False)

    @pl.when(gy < last)
    def _():
        high_side()

    @pl.when(gy < last - 1)
    def _():
        pl.semaphore_wait(far, far_count)

    @pl.when(gy == 0)
    def _():
        for copy in corners_down + [down]:
            copy.start()
        low_side(True)

    level = level_of()
    for owner in range(owners):
        outgoing[0, owner] = level[owner * portion : (owner + 1) * portion]

    deals = []
    for step in range(owners - 1, 0, -1):
        partner = partner_of(gy, step, owners)
        deals.append(
            pltpu.make_async_remote_copy(
                src_ref=outgoing.at[0, partner],
                dst_ref=gathered.at[gy],
                send_sem=deal_send.at[step - 1],
                recv_sem=deal_recv.at[step - 1],
                device_id=(gx, partner),
                device_id_type=MESH,
            )
        )
        deals[-1].start()
    gathered[gy] = outgoing[0, gy]

    late = [
        pltpu.make_async_remote_copy(
            src_ref=outgoing.at[1, owner],
            dst_ref=gathered.at[owners],
            send_sem=late_send.at[owner - 1],
            recv_sem=late_recv,
            device_id=(gx, owner),
            device_id_type=MESH,
        )
        for owner in range(1, owners)
    ]

    @pl.when(gy == 0)
    def _():
        wrap.wait_recv()
        first(low - 2)
        first(low - 3, (low - 4,))
        pair(pairs - 1, low - 2, own=False)
        level = level_of()
        for owner in range(owners):
            outgoing[1, owner] = level[owner * portion : (owner + 1) * portion]
        for copy in late:
            copy.start()
        gathered[owners] = outgoing[1, 0]

    @pl.when(gy == last)
    def _():
        high_side()

    for deal in deals:
        deal.wait_recv()

    @pl.when(gy > 0)
    def _():
        late[0].wait_recv()

    for copy in across + corners_up + corners_down + [up, down]:
        copy.wait_send()
    for deal in deals:
        deal.wait_send()

    @pl.when(gy == 0)
    def _():
        for copy in late:
            copy.wait_send()

    @pl.when(gy == last)
    def _():
        wrap.wait_send()


def finish(u_ref, v_ref, dealt, u_out, v_out, rebuilt_out, doubled, paired, rebuilt, sems):
    copies = [
        pltpu.make_async_copy(u_ref, u_out, sems.at[0]),
        pltpu.make_async_copy(v_ref, v_out, sems.at[1]),
    ]
    for copy in copies:
        copy.start()

    owners, portion = dealt.shape[0] - 1, dealt.shape[1]
    wide_in = lax.broadcasted_iota(jnp.int32, (LANES, 4 * LANES), 0)
    wide_out = lax.broadcasted_iota(jnp.int32, (LANES, 4 * LANES), 1)
    column_of = wide_in // 16 * 4 + wide_in % 4
    plane = wide_in // 4 % 4 == wide_out // LANES
    spreading = jnp.concatenate(
        [
            jnp.where(plane & (column_of == wide_out % LANES // 2), 0.5, 0.0),
            jnp.where(plane & (column_of // 2 == wide_out % LANES // 4), 0.125, 0.0),
        ],
        axis=0,
    ).astype(jnp.bfloat16)
    lane = lax.broadcasted_iota(jnp.int32, (portion, LANES), 1)
    even = lax.broadcasted_iota(jnp.int32, (portion, LANES), 0) % 2 == 0
    blocks = [dealt[owner] for owner in range(owners)]
    blocks[-1] = jnp.where(lane % 4 == 3, dealt[owners], blocks[-1])
    width, rows = rebuilt.shape[1], 2 * portion
    chunks = 4
    share = 8 // chunks
    for chunk in range(chunks):
        for h in range(chunk * share, (chunk + 1) * share):
            part = jnp.zeros((portion, LANES), jnp.float32)
            for owner in range(8):
                shift = (16 * (owner - h)) % LANES
                moved = pltpu.roll(blocks[owner], shift, 1) if shift else blocks[owner]
                part = jnp.where(lane // 16 == owner, moved, part)
            other = jnp.where(even, pltpu.roll(part, portion - 1, 0), pltpu.roll(part, 1, 0))
            total = part + other
            for twin in range(2):
                doubled[pl.ds(h * rows + twin, portion, stride=2), :] = part
                paired[pl.ds(h * rows + twin, portion, stride=2), :] = total
        span = slice(chunk * share * rows, (chunk + 1) * share * rows)
        high, low = split(jnp.concatenate([doubled[span, :], paired[span, :]], axis=1))
        whole = jnp.dot(high, spreading, preferred_element_type=jnp.float32)
        whole += jnp.dot(low, spreading, preferred_element_type=jnp.float32)
        for h in range(share):
            for z in range(4):
                base = ((chunk * share + h) * 4 + z) * rows
                rebuilt[base : base + rows, :] = whole[
                    h * rows : (h + 1) * rows, z * LANES : z * LANES + width
                ]
        size = share * 4 * rows
        copies.append(
            pltpu.make_async_copy(
                rebuilt.at[chunk * size : (chunk + 1) * size],
                rebuilt_out.at[chunk * size : (chunk + 1) * size],
                sems.at[2 + chunk],
            )
        )
        copies[-1].start()
    for copy in copies:
        copy.wait()


def tiled(field):
    planes, columns, extent = field.shape
    field = field.reshape(planes, columns, extent // LANES, LANES)
    return jnp.transpose(field, (0, 2, 1, 3)).reshape(-1, LANES)


def untiled(field, shape):
    planes, columns, extent = shape
    field = field.reshape(planes, extent // LANES, columns, LANES)
    return jnp.transpose(field, (0, 2, 1, 3)).reshape(shape)


def body(substrate, catalyst):
    planes, columns, extent = substrate.shape
    slabs_x, owners = lax.axis_size("gx"), lax.axis_size("gy")
    half, pairs, tiles = extent // 2, columns // 2, extent // LANES
    portion = half // owners
    values = 2 * planes * pairs
    fused = (
        planes == 16 and pairs == 4 and owners == 8 and values == LANES and portion % 8 == 0
    )
    dims = (planes, columns, extent, owners, slabs_x)
    f32 = jnp.float32
    flat = (planes * tiles * columns, LANES)
    vmem = pl.BlockSpec(memory_space=pltpu.VMEM)
    anywhere = pl.BlockSpec(memory_space=pl.ANY)
    u, v, dealt = pl.pallas_call(
        functools.partial(kernel, dims),
        out_shape=(
            pltpu.VMEM(flat, f32),
            pltpu.VMEM(flat, f32),
            pltpu.VMEM((owners + 1, portion, values), f32),
        ),
        in_specs=[anywhere] * 2,
        out_specs=(vmem,) * 3,
        scratch_shapes=[
            pltpu.VMEM((2,) + flat, f32),
            pltpu.VMEM((2, columns + 6, planes, extent), f32),
            pltpu.VMEM((2, columns + 6, planes, LANES), f32),
            pltpu.VMEM((planes, LANES), f32),
            pltpu.VMEM((2, planes, LANES), f32),
            pltpu.VMEM((2, 2, planes, LANES), f32),
            pltpu.VMEM((2, columns + 6, planes, extent + LANES), f32),
            pltpu.VMEM((tiles, values, LANES), f32),
            pltpu.VMEM((2, owners, portion, values), f32),
            pltpu.SemaphoreType.DMA((2,)),
            pltpu.SemaphoreType.DMA((9,)),
            pltpu.SemaphoreType.DMA((9,)),
            pltpu.SemaphoreType.DMA((owners - 1,)),
            pltpu.SemaphoreType.DMA((owners - 1,)),
            pltpu.SemaphoreType.DMA((owners - 1,)),
            pltpu.SemaphoreType.DMA,
            pltpu.SemaphoreType.REGULAR,
        ],
        compiler_params=pltpu.CompilerParams(collective_id=0, has_side_effects=True),
    )(tiled(substrate), tiled(catalyst))
    rows, width = 2 * portion, columns * owners
    if fused:
        u, v, dealt = (
            pltpu.with_memory_space_constraint(x, pltpu.VMEM) for x in (u, v, dealt)
        )
        u, v, rebuilt = pl.pallas_call(
            finish,
            out_shape=(
                jax.ShapeDtypeStruct(flat, f32),
                jax.ShapeDtypeStruct(flat, f32),
                jax.ShapeDtypeStruct((2 * planes * rows, width), f32),
            ),
            in_specs=[vmem] * 3,
            out_specs=(anywhere,) * 3,
            scratch_shapes=[
                pltpu.VMEM((8 * rows, LANES), f32),
                pltpu.VMEM((8 * rows, LANES), f32),
                pltpu.VMEM((2 * planes * rows, width), f32),
                pltpu.SemaphoreType.DMA((6,)),
            ],
        )(u, v, dealt)
        rebuilt = rebuilt.reshape(2, planes, rows, width)
    else:
        level = dealt.reshape(owners + 1, portion, 2, planes, pairs)
        latest = jnp.concatenate([level[owners - 1, ..., :-1], level[owners, ..., -1:]], axis=-1)
        level = jnp.concatenate([level[: owners - 1], latest[None]], axis=0)
        level = jnp.transpose(level, (2, 3, 1, 0, 4)).reshape(2, planes, portion // 2, 2, columns * owners // 4, 2)
        coarse = 0.25 * jnp.sum(level, axis=(3, 5), keepdims=True)
        blend = (coarse + 0.5 * (level - coarse)).reshape(2, planes, portion, columns * owners // 2)
        rebuilt = jnp.repeat(jnp.repeat(blend, 2, axis=2), 2, axis=3)
    return untiled(u, substrate.shape), untiled(v, substrate.shape), rebuilt


def solution(mesh):
    in_specs = (P(None, "gy", "gx"), P(None, "gy", "gx"))
    out_specs = (P(None, "gy", "gx"), P(None, "gy", "gx"), P(None, None, ("gx", "gy"), None))
    return jax.shard_map(body, mesh=mesh, in_specs=in_specs, out_specs=out_specs, check_vma=False)
```

time: 18.8 us -> 17.6 us (0.936)
  Pallas kernels: 18 us -> 16.8 us
    pallas_call x1, Pallas kernels: 16.9 us -> 15.5 us  [body(): pl.pallas_call(functools.partial(kernel, dims), out_shape=(pltpu.VMEM(fla...]
where the time goes in v2:
time: 17.6 us; the launch traced here: 17.5 us
  Pallas kernels  16.8 us (95%)
  between operations  0.64 us (4%)
    pallas_call x1, Pallas kernels, body(): pl.pallas_call(functools.partial(kernel, dims), out_shape=(pltpu.VMEM(fla...  15.5 us
    pallas_call x1, Pallas kernels, body(): pl.pallas_call(finish, out_shape=(jax.ShapeDtypeStruct(flat, f32), jax.Sh...  1.3 us

profile of v2, /device:TPU:0, one launch (start us, length us, event | category | flops | bytes accessed | tf_op | source)
XLA Modules:
  0.0 17.5 jit_solution(13612645781763043384)
XLA Ops:
  0.6 15.5 %shard_map.49 = (f32[256,128]{1,0:T(8,128)S(1)}, f32[256,128]{1,0:T(8,128)S(1)}, f32[9,16,128]{2,1,0:T(8,128)S(1)}) custom-call(f32[256,128]{1,0:T(8,128)} %bitcast.21, f32[256,128]{1,0:T(8,128)} %bitcast.22), custom_call_target="tpu_custom_call" | custom-call | tf_op jit(solution)/shard_map/pallas_call | solution.py:420
  16.2 1.3 %shard_map.50 = (f32[256,128]{1,0:T(8,128)}, f32[256,128]{1,0:T(8,128)}, f32[1024,64]{1,0:T(8,128)}) custom-call(f32[256,128]{1,0:T(8,128)S(1)} %get-tuple-element.9.u_ref, f32[256,128]{1,0:T(8,128)S(1)} %get-tuple-element.10.v_ref, f32[9,16,128]{2,1,0:T(8,128)S(1)} %get-tuple-element.11.dealt), custom_call_target="tpu_custom_call" | custom-call | tf_op jit(solution)/shard_map/pallas_call | solution.py:455

commit v3 on v2

--- a/solution.py
+++ b/solution.py
@@ -47,21 +47,18 @@
     return total - 6.0 * here
 
 
-def partner_of(me, step, size):
-    if size & (size - 1):
-        return lax.rem(me + step, size)
-    partner = me + step
-    for bit in range(size.bit_length() - 1):
-        if step >> bit & 1:
-            partner = partner - 2 * (1 << bit) * lax.rem(me // (1 << bit), 2)
-    return partner
-
-
 def kernel(dims, *refs):
     planes, columns, extent, owners, slabs_x = dims
     (u_ref, v_ref, u_out, v_out, gathered, loaded, state, edge, packed, got, corner, middle, sums, outgoing,
      load_sem, send_sem, recv_sem, deal_send, deal_recv, late_send, late_recv, far) = refs
     tiles, pairs, last = extent // LANES, columns // 2, owners - 1
+    half = extent // 2
+    portion = half // owners
+    widths = (LANES, extent) if tiles > 1 else (extent,)
+    dealt_to = [(width - 2) // (2 * portion) for width in widths[:-1]] + [owners]
+    spans = list(zip((0,) + widths[:-1], widths))
+    shares = list(zip([0] + dealt_to[:-1], dealt_to))
+    parts = range(len(widths))
     gx, gy = lax.axis_index("gx"), lax.axis_index("gy")
     at_top, at_bottom = gy // last, (last - gy) // last
 
@@ -132,23 +129,26 @@
             device_id_type=MESH,
         )
 
-    up = send(0, state.at[:, high - 2 : high], state.at[:, low - 2 : low], gx, along_of[0])
-    down = send(1, state.at[:, low : low + 2], state.at[:, high : high + 2], gx, along_of[1])
-    wrap = send(2, state.at[:, high - 4 : high - 2], state.at[:, low - 4 : low - 2], gx, along_of[0])
-    across = [send(3 + side, packed, got.at[side], across_of[side], gy) for side in range(2)]
-    corners_up = [send(5 + side, packed, corner.at[0, side], across_of[side], along_of[0]) for side in range(2)]
-    corners_down = [send(7 + side, packed, corner.at[1, side], across_of[side], along_of[1]) for side in range(2)]
-    for copy in across + corners_up + [up]:
-        copy.start()
-
-    @pl.when(gy > 0)
-    def _():
-        for copy in corners_down + [down]:
-            copy.start()
+    def columns_of(first_column, count, part):
+        return state.at[:, first_column : first_column + count, :, slice(*spans[part])]
+
+    across = [send(side, packed, got.at[side], across_of[side], gy) for side in range(2)]
+    corners_up = [send(2 + side, packed, corner.at[0, side], across_of[side], along_of[0]) for side in range(2)]
+    corners_down = [send(4 + side, packed, corner.at[1, side], across_of[side], along_of[1]) for side in range(2)]
+    up, down, wrap = [
+        [
+            send(6 + 3 * part + kind, columns_of(source, 2, part), columns_of(target, 2, part), gx, along_of[way])
+            for part in parts
+        ]
+        for kind, source, target, way in (
+            (0, high - 2, low - 2, 0),
+            (1, low, high, 1),
+            (2, high - 4, low - 4, 0),
+        )
+    ]
 
     @pl.when(gy == last)
     def _():
-        wrap.start()
         for x in across_of:
             greet(far, x, 0)
 
@@ -158,7 +158,25 @@
         def _():
             greet(far, gx, peer)
 
-    half = extent // 2
+    for copy in across + corners_up:
+        copy.start()
+
+    @pl.when(gy > 0)
+    def _():
+        for copy in corners_down:
+            copy.start()
+
+    for part in parts:
+        up[part].start()
+
+        @pl.when(gy > 0)
+        def _():
+            down[part].start()
+
+        @pl.when(gy == last)
+        def _():
+            wrap[part].start()
+
     row = lax.broadcasted_iota(jnp.int32, (half, extent), 0)
     fine = lax.broadcasted_iota(jnp.int32, (half, extent), 1)
     to_level = jnp.where(fine // 2 == row, 0.25, 0.0).astype(jnp.bfloat16)
@@ -178,155 +196,182 @@
     for column in range(columns):
         place(low + column, both, column)
 
-    def wide(field, c, outer=()):
+    def wide(field, c, width, outer=()):
         tail = jnp.zeros((planes, LANES), jnp.float32) if c in outer else edge[field, c]
-        return jnp.concatenate([state[field, c], tail], axis=1)
-
-    def first(c, outer=()):
-        u, v = wide(0, c), wide(1, c)
-        su = spread_of(wide(0, c - 1, outer), u, wide(0, c + 1, outer))
-        sv = spread_of(wide(1, c - 1, outer), v, wide(1, c + 1, outer))
-        middle[0, c], middle[1, c] = react(u, v, su, sv)
-
-    def second(c):
-        u, v = middle[0, c], middle[1, c]
-        su = spread_of(middle[0, c - 1], u, middle[0, c + 1])
-        sv = spread_of(middle[1, c - 1], v, middle[1, c + 1])
-        return react(u[:, :extent], v[:, :extent], su[:, :extent], sv[:, :extent])
-
-    def pair(k, c, own=True):
-        new = [second(c), second(c + 1)]
+        return jnp.concatenate([state[field, c, :, :width], tail], axis=1)
+
+    def first(c, width, outer=()):
+        u, v = wide(0, c, width), wide(1, c, width)
+        su = spread_of(wide(0, c - 1, width, outer), u, wide(0, c + 1, width, outer))
+        sv = spread_of(wide(1, c - 1, width, outer), v, wide(1, c + 1, width, outer))
+        for field, new in enumerate(react(u, v, su, sv)):
+            middle[field, c, :, :width] = new[:, :width]
+            middle[field, c, :, extent:] = new[:, width:]
+
+    def half_way(field, c, width):
+        return jnp.concatenate([middle[field, c, :, :width], middle[field, c, :, extent:]], axis=1)
+
+    def second(c, width):
+        u, v = half_way(0, c, width), half_way(1, c, width)
+        su = spread_of(half_way(0, c - 1, width), u, half_way(0, c + 1, width))
+        sv = spread_of(half_way(1, c - 1, width), v, half_way(1, c + 1, width))
+        return react(u[:, :width], v[:, :width], su[:, :width], sv[:, :width])
+
+    def pair(k, c, width=extent, own=True):
+        new = [second(c, width), second(c + 1, width)]
         for field, out in enumerate((u_out, v_out)):
-            for tile in range(tiles):
+            for tile in range(width // LANES):
                 lanes = slice(tile * LANES, (tile + 1) * LANES)
-                parts = [new[i][field][:, lanes] for i in range(2)]
+                both_of = [new[i][field][:, lanes] for i in range(2)]
                 if own:
                     for i in range(2):
                         rows = pl.ds(tile * columns + c - low + i, planes, stride=tiles * columns)
-                        out[rows, :] = parts[i]
+                        out[rows, :] = both_of[i]
                 rows = pl.ds(field * planes * pairs + k, planes, stride=pairs)
-                sums[tile, rows, :] = parts[0] + parts[1]
-
-    def low_side(wrapped):
-        up.wait_recv()
-        for copy in corners_up:
-            copy.wait_recv()
-        beyond = merged(corner[0, 0], corner[0, 1])
-        for step in range(1, 4 if wrapped else 2):
-            place(low - step, beyond, columns - step)
-        first(low)
-        first(low - 1, () if wrapped else (low - 2,))
-        pair(0, low)
-
-    def high_side():
-        down.wait_recv()
+                sums[tile, rows, :] = both_of[0] + both_of[1]
+
+    final = len(widths) - 1
+
+    def low_side(part, wrapped):
+        width = widths[part]
+        up[part].wait_recv()
+        if part == 0:
+            for copy in corners_up:
+                copy.wait_recv()
+            beyond = merged(corner[0, 0], corner[0, 1])
+            for step in range(1, 4 if wrapped else 2):
+                place(low - step, beyond, columns - step)
+        first(low, width)
+        first(low - 1, width, () if wrapped else (low - 2,))
+        pair(0, low, width, own=part == final)
+
+    def high_side(part):
+        width = widths[part]
+        down[part].wait_recv()
+        if part == 0:
+            for copy in corners_down:
+                copy.wait_recv()
+            place(high, merged(corner[1, 0], corner[1, 1]), 0)
+        first(high - 1, width)
+        first(high, width, (high + 1,))
+        pair(pairs - 1, high - 2, width, own=part == final)
+
+    def level_of(slot, part):
+        width = widths[part]
+        contract = (((1,), (1,)), ((), ()))
+        taking = to_level[: width // 2, :width]
+        upper, lower = split(jnp.concatenate([sums[tile] for tile in range(width // LANES)], axis=1))
+        level = lax.dot_general(taking, upper, contract, preferred_element_type=jnp.float32)
+        level += lax.dot_general(taking, lower, contract, preferred_element_type=jnp.float32)
+        for owner in range(*shares[part]):
+            outgoing[slot, owner] = level[owner * portion : (owner + 1) * portion]
+
+    def deal(slot, owner, target, sender, receiver):
+        return pltpu.make_async_remote_copy(
+            src_ref=outgoing.at[slot, owner],
+            dst_ref=gathered.at[target],
+            send_sem=sender,
+            recv_sem=receiver,
+            device_id=(gx, owner),
+            device_id_type=MESH,
+        )
+
+    deals = [deal(0, owner, gy, deal_send.at[owner], deal_recv.at[gy]) for owner in range(owners)]
+    late = [None] + [deal(1, owner, owners, late_send.at[owner], late_recv) for owner in range(1, owners)]
+
+    for c in range(low + 1, high - 1):
+        first(c, extent)
+    for k in range(1, pairs - 1):
+        pair(k, low + 2 * k)
+
+    for part in parts:
+
+        @pl.when(gy > 0)
+        def _():
+            low_side(part, False)
+
+        @pl.when(gy < last)
+        def _():
+            high_side(part)
+
+        if part == 0:
+
+            @pl.when(gy < last - 1)
+            def _():
+                pl.semaphore_wait(far, far_count)
+
+        @pl.when(gy == 0)
+        def _():
+            if part == 0:
+                for copy in corners_down + down:
+                    copy.start()
+            low_side(part, True)
+
+        level_of(0, part)
+        for owner in range(*shares[part]):
+
+            @pl.when(owner != gy)
+            def _():
+                deals[owner].start()
+
+        @pl.when(gy == 0)
+        def _():
+            wrap[part].wait_recv()
+            width = widths[part]
+            first(low - 2, width)
+            first(low - 3, width, (low - 4,))
+            pair(pairs - 1, low - 2, width, own=False)
+            level_of(1, part)
+            for owner in range(*shares[part]):
+                if owner:
+                    late[owner].start()
+
+    gathered[gy] = outgoing[0, gy]
+
+    @pl.when(gy == 0)
+    def _():
+        gathered[owners] = outgoing[1, 0]
+
+    @pl.when(gy == last)
+    def _():
+        for part in parts:
+            if part < final:
+                down[part].wait_recv()
         for copy in corners_down:
             copy.wait_recv()
         place(high, merged(corner[1, 0], corner[1, 1]), 0)
-        first(high - 1)
-        first(high, (high + 1,))
+        down[final].wait_recv()
+        first(high - 1, extent)
+        first(high, extent, (high + 1,))
         pair(pairs - 1, high - 2)
 
-    def level_of():
-        contract = (((1,), (1,)), ((), ()))
-        upper, lower = split(jnp.concatenate([sums[tile] for tile in range(tiles)], axis=1))
-        level = lax.dot_general(to_level, upper, contract, preferred_element_type=jnp.float32)
-        return level + lax.dot_general(to_level, lower, contract, preferred_element_type=jnp.float32)
-
-    portion = half // owners
-
-    for c in range(low + 1, high - 1):
-        first(c)
-    for k in range(1, pairs - 1):
-        pair(k, low + 2 * k)
+    for sender in range(owners):
+
+        @pl.when(sender != gy)
+        def _():
+            deal(0, sender, sender, deal_send.at[sender], deal_recv.at[sender]).wait_recv()
 
     @pl.when(gy > 0)
     def _():
-        low_side(False)
-
-    @pl.when(gy < last)
-    def _():
-        high_side()
-
-    @pl.when(gy < last - 1)
-    def _():
-        pl.semaphore_wait(far, far_count)
+        late[1].wait_recv()
+
+    for copy in across + corners_up + corners_down + up + down:
+        copy.wait_send()
+    for owner in range(owners):
+
+        @pl.when(owner != gy)
+        def _():
+            deals[owner].wait_send()
 
     @pl.when(gy == 0)
     def _():
-        for copy in corners_down + [down]:
-            copy.start()
-        low_side(True)
-
-    level = level_of()
-    for owner in range(owners):
-        outgoing[0, owner] = level[owner * portion : (owner + 1) * portion]
-
-    deals = []
-    for step in range(owners - 1, 0, -1):
-        partner = partner_of(gy, step, owners)
-        deals.append(
-            pltpu.make_async_remote_copy(
-                src_ref=outgoing.at[0, partner],
-                dst_ref=gathered.at[gy],
-                send_sem=deal_send.at[step - 1],
-                recv_sem=deal_recv.at[step - 1],
-                device_id=(gx, partner),
-                device_id_type=MESH,
-            )
-        )
-        deals[-1].start()
-    gathered[gy] = outgoing[0, gy]
-
-    late = [
-        pltpu.make_async_remote_copy(
-            src_ref=outgoing.at[1, owner],
-            dst_ref=gathered.at[owners],
-            send_sem=late_send.at[owner - 1],
-            recv_sem=late_recv,
-            device_id=(gx, owner),
-            device_id_type=MESH,
-        )
-        for owner in range(1, owners)
-    ]
-
-    @pl.when(gy == 0)
-    def _():
-        wrap.wait_recv()
-        first(low - 2)
-        first(low - 3, (low - 4,))
-        pair(pairs - 1, low - 2, own=False)
-        level = level_of()
-        for owner in range(owners):
-            outgoing[1, owner] = level[owner * portion : (owner + 1) * portion]
-        for copy in late:
-            copy.start()
-        gathered[owners] = outgoing[1, 0]
+        for copy in late[1:]:
+            copy.wait_send()
 
     @pl.when(gy == last)
     def _():
-        high_side()
-
-    for deal in deals:
-        deal.wait_recv()
-
-    @pl.when(gy > 0)
-    def _():
-        late[0].wait_recv()
-
-    for copy in across + corners_up + corners_down + [up, down]:
-        copy.wait_send()
-    for deal in deals:
-        deal.wait_send()
-
-    @pl.when(gy == 0)
-    def _():
-        for copy in late:
+        for copy in wrap:
             copy.wait_send()
-
-    @pl.when(gy == last)
-    def _():
-        wrap.wait_send()
 
 
 def finish(u_ref, v_ref, dealt, u_out, v_out, rebuilt_out, doubled, paired, rebuilt, sems):
@@ -437,11 +482,11 @@
             pltpu.VMEM((tiles, values, LANES), f32),
             pltpu.VMEM((2, owners, portion, values), f32),
             pltpu.SemaphoreType.DMA((2,)),
-            pltpu.SemaphoreType.DMA((9,)),
-            pltpu.SemaphoreType.DMA((9,)),
-            pltpu.SemaphoreType.DMA((owners - 1,)),
-            pltpu.SemaphoreType.DMA((owners - 1,)),
-            pltpu.SemaphoreType.DMA((owners - 1,)),
+            pltpu.SemaphoreType.DMA((12,)),
+            pltpu.SemaphoreType.DMA((12,)),
+            pltpu.SemaphoreType.DMA((owners,)),
+            pltpu.SemaphoreType.DMA((owners,)),
+            pltpu.SemaphoreType.DMA((owners,)),
             pltpu.SemaphoreType.DMA,
             pltpu.SemaphoreType.REGULAR,
         ],

time: 17.6 us -> 16.8 us (0.955)
  Pallas kernels: 16.8 us -> 16 us
    pallas_call x1, Pallas kernels: 15.5 us -> 14.7 us  [body(): pl.pallas_call(functools.partial(kernel, dims), out_shape=(pltpu.VMEM(fla...]
where the time goes in v3:
time: 16.8 us; the launch traced here: 16.7 us
  Pallas kernels  16 us (95%)
  between operations  0.64 us (4%)
    pallas_call x1, Pallas kernels, body(): pl.pallas_call(functools.partial(kernel, dims), out_shape=(pltpu.VMEM(fla...  14.7 us
    pallas_call x1, Pallas kernels, body(): pl.pallas_call(finish, out_shape=(jax.ShapeDtypeStruct(flat, f32), jax.Sh...  1.3 us

profile of v3, /device:TPU:0, one launch (start us, length us, event | category | flops | bytes accessed | tf_op | source)
XLA Modules:
  0.0 16.7 jit_solution(7611260958416307935)
XLA Ops:
  0.6 14.7 %shard_map.49 = (f32[256,128]{1,0:T(8,128)S(1)}, f32[256,128]{1,0:T(8,128)S(1)}, f32[9,16,128]{2,1,0:T(8,128)S(1)}) custom-call(f32[256,128]{1,0:T(8,128)} %bitcast.21, f32[256,128]{1,0:T(8,128)} %bitcast.22), custom_call_target="tpu_custom_call" | custom-call | tf_op jit(solution)/shard_map/pallas_call | solution.py:465
  15.4 1.3 %shard_map.50 = (f32[256,128]{1,0:T(8,128)}, f32[256,128]{1,0:T(8,128)}, f32[1024,64]{1,0:T(8,128)}) custom-call(f32[256,128]{1,0:T(8,128)S(1)} %get-tuple-element.9.u_ref, f32[256,128]{1,0:T(8,128)S(1)} %get-tuple-element.10.v_ref, f32[9,16,128]{2,1,0:T(8,128)S(1)} %get-tuple-element.11.dealt), custom_call_target="tpu_custom_call" | custom-call | tf_op jit(solution)/shard_map/pallas_call | solution.py:500

commit v4 on v3

--- a/solution.py
+++ b/solution.py
@@ -50,7 +50,7 @@
 def kernel(dims, *refs):
     planes, columns, extent, owners, slabs_x = dims
     (u_ref, v_ref, u_out, v_out, gathered, loaded, state, edge, packed, got, corner, middle, sums, outgoing,
-     load_sem, send_sem, recv_sem, deal_send, deal_recv, late_send, late_recv, far) = refs
+     load_sem, send_sem, recv_sem, far) = refs
     tiles, pairs, last = extent // LANES, columns // 2, owners - 1
     half = extent // 2
     portion = half // owners
@@ -88,13 +88,12 @@
     far_count = last - gy - 1 + 2 * at_bottom
 
     loads = [
-        pltpu.make_async_copy(source, loaded.at[field], load_sem.at[field])
+        pltpu.make_async_copy(source, loaded.at[field], load_sem)
         for field, source in enumerate((u_ref, v_ref))
     ]
     for load in loads:
         load.start()
-    for load in loads:
-        load.wait()
+    pltpu.make_async_copy(loaded, loaded, load_sem).wait()
 
     low = 4
     high = low + columns
@@ -119,33 +118,40 @@
 
     pl.semaphore_wait(barrier, near_count)
 
-    def send(number, source, target, x, y):
+    def send(sender, receiver, source, target, x, y):
         return pltpu.make_async_remote_copy(
             src_ref=source,
             dst_ref=target,
-            send_sem=send_sem.at[number],
-            recv_sem=recv_sem.at[number],
+            send_sem=send_sem.at[sender],
+            recv_sem=recv_sem.at[receiver],
             device_id=(x, y),
             device_id_type=MESH,
         )
 
+    def wait_sent(sender, ref):
+        send(sender, 0, ref, ref, gx, gy).wait_send()
+
+    def wait_got(receiver, ref):
+        send(0, receiver, ref, ref, gx, gy).wait_recv()
+
     def columns_of(first_column, count, part):
         return state.at[:, first_column : first_column + count, :, slice(*spans[part])]
 
-    across = [send(side, packed, got.at[side], across_of[side], gy) for side in range(2)]
-    corners_up = [send(2 + side, packed, corner.at[0, side], across_of[side], along_of[0]) for side in range(2)]
-    corners_down = [send(4 + side, packed, corner.at[1, side], across_of[side], along_of[1]) for side in range(2)]
+    across = [send(0, 0, packed, got.at[side], across_of[side], gy) for side in range(2)]
+    corners_up = [send(0, 1, packed, corner.at[0, side], across_of[side], along_of[0]) for side in range(2)]
+    corners_down = [send(0, 2, packed, corner.at[1, side], across_of[side], along_of[1]) for side in range(2)]
     up, down, wrap = [
         [
-            send(6 + 3 * part + kind, columns_of(source, 2, part), columns_of(target, 2, part), gx, along_of[way])
+            send(sender, receiver + 3 * part, columns_of(source, 2, part), columns_of(target, 2, part), gx, along_of[way])
             for part in parts
         ]
-        for kind, source, target, way in (
-            (0, high - 2, low - 2, 0),
-            (1, low, high, 1),
-            (2, high - 4, low - 4, 0),
+        for sender, receiver, source, target, way in (
+            (1, 1, high - 2, low - 2, 0),
+            (1, 2, low, high, 1),
+            (2, 3, high - 4, low - 4, 0),
         )
     ]
+    dealt_recv = 1 + 3 * len(widths)
 
     @pl.when(gy == last)
     def _():
@@ -167,22 +173,27 @@
             copy.start()
 
     for part in parts:
-        up[part].start()
-
-        @pl.when(gy > 0)
+
+        @pl.when(gy < last)
+        def _():
+            up[part].start()
+
+        @pl.when((gy > 0) & (gy < last))
         def _():
             down[part].start()
 
         @pl.when(gy == last)
         def _():
-            wrap[part].start()
+            copies = [up[part], wrap[part]]
+            copies.insert(0 if part == 0 else 2, down[part])
+            for copy in copies:
+                copy.start()
 
     row = lax.broadcasted_iota(jnp.int32, (half, extent), 0)
     fine = lax.broadcasted_iota(jnp.int32, (half, extent), 1)
     to_level = jnp.where(fine // 2 == row, 0.25, 0.0).astype(jnp.bfloat16)
 
-    for copy in across:
-        copy.wait_recv()
+    wait_got(0, got)
 
     def merged(below, above):
         return jnp.where(lax.rem(lane, 4) < 2, above, below)
@@ -217,7 +228,7 @@
         sv = spread_of(half_way(1, c - 1, width), v, half_way(1, c + 1, width))
         return react(u[:, :width], v[:, :width], su[:, :width], sv[:, :width])
 
-    def pair(k, c, width=extent, own=True):
+    def pair(k, c, width=extent, own=True, slot=0):
         new = [second(c, width), second(c + 1, width)]
         for field, out in enumerate((u_out, v_out)):
             for tile in range(width // LANES):
@@ -228,16 +239,20 @@
                         rows = pl.ds(tile * columns + c - low + i, planes, stride=tiles * columns)
                         out[rows, :] = both_of[i]
                 rows = pl.ds(field * planes * pairs + k, planes, stride=pairs)
-                sums[tile, rows, :] = both_of[0] + both_of[1]
+                sums[slot, tile, rows, :] = both_of[0] + both_of[1]
 
     final = len(widths) - 1
+
+    def wait_side(way, part):
+        if part == 0:
+            wait_got(1 + way, state.at[:, 0:3, :, :LANES])
+        else:
+            up[part].wait_recv() if way == 0 else down[part].wait_recv()
 
     def low_side(part, wrapped):
         width = widths[part]
-        up[part].wait_recv()
+        wait_side(0, part)
         if part == 0:
-            for copy in corners_up:
-                copy.wait_recv()
             beyond = merged(corner[0, 0], corner[0, 1])
             for step in range(1, 4 if wrapped else 2):
                 place(low - step, beyond, columns - step)
@@ -247,37 +262,34 @@
 
     def high_side(part):
         width = widths[part]
-        down[part].wait_recv()
+        wait_side(1, part)
         if part == 0:
-            for copy in corners_down:
-                copy.wait_recv()
             place(high, merged(corner[1, 0], corner[1, 1]), 0)
         first(high - 1, width)
         first(high, width, (high + 1,))
         pair(pairs - 1, high - 2, width, own=part == final)
 
-    def level_of(slot, part):
+    def level_of(part, slots):
         width = widths[part]
         contract = (((1,), (1,)), ((), ()))
         taking = to_level[: width // 2, :width]
-        upper, lower = split(jnp.concatenate([sums[tile] for tile in range(width // LANES)], axis=1))
+        values = jnp.concatenate(
+            [jnp.concatenate([sums[slot, tile] for tile in range(width // LANES)], axis=1) for slot in range(slots)],
+            axis=0,
+        )
+        upper, lower = split(values)
         level = lax.dot_general(taking, upper, contract, preferred_element_type=jnp.float32)
         level += lax.dot_general(taking, lower, contract, preferred_element_type=jnp.float32)
+        size = sums.shape[2]
         for owner in range(*shares[part]):
-            outgoing[slot, owner] = level[owner * portion : (owner + 1) * portion]
-
-    def deal(slot, owner, target, sender, receiver):
-        return pltpu.make_async_remote_copy(
-            src_ref=outgoing.at[slot, owner],
-            dst_ref=gathered.at[target],
-            send_sem=sender,
-            recv_sem=receiver,
-            device_id=(gx, owner),
-            device_id_type=MESH,
-        )
-
-    deals = [deal(0, owner, gy, deal_send.at[owner], deal_recv.at[gy]) for owner in range(owners)]
-    late = [None] + [deal(1, owner, owners, late_send.at[owner], late_recv) for owner in range(1, owners)]
+            for slot in range(slots):
+                outgoing[slot, owner] = level[
+                    owner * portion : (owner + 1) * portion, slot * size : (slot + 1) * size
+                ]
+
+    def deal(slot, owner):
+        target = owners if slot else gy
+        return send(3 + slot, dealt_recv, outgoing.at[slot, owner], gathered.at[target], gx, owner)
 
     for c in range(low + 1, high - 1):
         first(c, extent)
@@ -307,71 +319,58 @@
                     copy.start()
             low_side(part, True)
 
-        level_of(0, part)
-        for owner in range(*shares[part]):
-
-            @pl.when(owner != gy)
-            def _():
-                deals[owner].start()
-
-        @pl.when(gy == 0)
-        def _():
             wrap[part].wait_recv()
             width = widths[part]
             first(low - 2, width)
             first(low - 3, width, (low - 4,))
-            pair(pairs - 1, low - 2, width, own=False)
-            level_of(1, part)
+            pair(pairs - 1, low - 2, width, own=False, slot=1)
+            level_of(part, 2)
             for owner in range(*shares[part]):
                 if owner:
-                    late[owner].start()
+                    deal(0, owner).start()
+                    deal(1, owner).start()
+
+        @pl.when(gy > 0)
+        def _():
+            level_of(part, 1)
+            for owner in range(*shares[part]):
+
+                @pl.when(owner != gy)
+                def _():
+                    deal(0, owner).start()
 
     gathered[gy] = outgoing[0, gy]
 
-    @pl.when(gy == 0)
-    def _():
-        gathered[owners] = outgoing[1, 0]
-
     @pl.when(gy == last)
     def _():
-        for part in parts:
-            if part < final:
-                down[part].wait_recv()
-        for copy in corners_down:
-            copy.wait_recv()
-        place(high, merged(corner[1, 0], corner[1, 1]), 0)
-        down[final].wait_recv()
+        for part in parts[:-1]:
+            wait_side(1, part)
+            if part == 0:
+                place(high, merged(corner[1, 0], corner[1, 1]), 0)
+        wait_side(1, final)
+        if final == 0:
+            place(high, merged(corner[1, 0], corner[1, 1]), 0)
         first(high - 1, extent)
         first(high, extent, (high + 1,))
         pair(pairs - 1, high - 2)
 
-    for sender in range(owners):
-
-        @pl.when(sender != gy)
-        def _():
-            deal(0, sender, sender, deal_send.at[sender], deal_recv.at[sender]).wait_recv()
+    @pl.when(gy == 0)
+    def _():
+        gathered[owners] = outgoing[1, 0]
+        wait_got(dealt_recv, gathered.at[1:owners])
+        wait_sent(4, outgoing.at[1, 1:])
 
     @pl.when(gy > 0)
     def _():
-        late[1].wait_recv()
-
-    for copy in across + corners_up + corners_down + up + down:
-        copy.wait_send()
-    for owner in range(owners):
-
-        @pl.when(owner != gy)
-        def _():
-            deals[owner].wait_send()
-
-    @pl.when(gy == 0)
-    def _():
-        for copy in late[1:]:
-            copy.wait_send()
+        wait_got(dealt_recv, gathered.at[:owners])
+
+    wait_sent(0, state.at[:, 0:3, :, :LANES])
+    wait_sent(1, state.at[:, 0:4])
+    wait_sent(3, outgoing.at[0, 1:])
 
     @pl.when(gy == last)
     def _():
-        for copy in wrap:
-            copy.wait_send()
+        wait_sent(2, state.at[:, 0:2])
 
 
 def finish(u_ref, v_ref, dealt, u_out, v_out, rebuilt_out, doubled, paired, rebuilt, sems):
@@ -428,11 +427,11 @@
             pltpu.make_async_copy(
                 rebuilt.at[chunk * size : (chunk + 1) * size],
                 rebuilt_out.at[chunk * size : (chunk + 1) * size],
-                sems.at[2 + chunk],
+                sems.at[2],
             )
         )
         copies[-1].start()
-    for copy in copies:
+    for copy in copies[:2] + [pltpu.make_async_copy(rebuilt, rebuilt_out, sems.at[2])]:
         copy.wait()
 
 
@@ -479,15 +478,11 @@
             pltpu.VMEM((2, planes, LANES), f32),
             pltpu.VMEM((2, 2, planes, LANES), f32),
             pltpu.VMEM((2, columns + 6, planes, extent + LANES), f32),
-            pltpu.VMEM((tiles, values, LANES), f32),
+            pltpu.VMEM((2, tiles, values, LANES), f32),
             pltpu.VMEM((2, owners, portion, values), f32),
-            pltpu.SemaphoreType.DMA((2,)),
-            pltpu.SemaphoreType.DMA((12,)),
-            pltpu.SemaphoreType.DMA((12,)),
-            pltpu.SemaphoreType.DMA((owners,)),
-            pltpu.SemaphoreType.DMA((owners,)),
-            pltpu.SemaphoreType.DMA((owners,)),
             pltpu.SemaphoreType.DMA,
+            pltpu.SemaphoreType.DMA((5,)),
+            pltpu.SemaphoreType.DMA((8 if tiles > 1 else 5,)),
             pltpu.SemaphoreType.REGULAR,
         ],
         compiler_params=pltpu.CompilerParams(collective_id=0, has_side_effects=True),
@@ -510,7 +505,7 @@
                 pltpu.VMEM((8 * rows, LANES), f32),
                 pltpu.VMEM((8 * rows, LANES), f32),
                 pltpu.VMEM((2 * planes * rows, width), f32),
-                pltpu.SemaphoreType.DMA((6,)),
+                pltpu.SemaphoreType.DMA((3,)),
             ],
         )(u, v, dealt)
         rebuilt = rebuilt.reshape(2, planes, rows, width)

time: 16.8 us -> 16.6 us (0.988)
  Pallas kernels: 16 us -> 15.8 us
    pallas_call x1, Pallas kernels: 14.7 us -> 14.5 us  [body(): pl.pallas_call(functools.partial(kernel, dims), out_shape=(pltpu.VMEM(fla...]
where the time goes in v4:
time: 16.6 us; the launch traced here: 16.4 us
  Pallas kernels  15.8 us (95%)
  between operations  0.64 us (4%)
    pallas_call x1, Pallas kernels, body(): pl.pallas_call(functools.partial(kernel, dims), out_shape=(pltpu.VMEM(fla...  14.5 us
    pallas_call x1, Pallas kernels, body(): pl.pallas_call(finish, out_shape=(jax.ShapeDtypeStruct(flat, f32), jax.Sh...  1.27 us

profile of v4, /device:TPU:0, one launch (start us, length us, event | category | flops | bytes accessed | tf_op | source)
XLA Modules:
  0.0 16.4 jit_solution(7298009844609839172)
XLA Ops:
  0.6 14.5 %shard_map.49 = (f32[256,128]{1,0:T(8,128)S(1)}, f32[256,128]{1,0:T(8,128)S(1)}, f32[9,16,128]{2,1,0:T(8,128)S(1)}) custom-call(f32[256,128]{1,0:T(8,128)} %bitcast.21, f32[256,128]{1,0:T(8,128)} %bitcast.22), custom_call_target="tpu_custom_call" | custom-call | tf_op jit(solution)/shard_map/pallas_call | solution.py:464
  15.1 1.3 %shard_map.50 = (f32[256,128]{1,0:T(8,128)}, f32[256,128]{1,0:T(8,128)}, f32[1024,64]{1,0:T(8,128)}) custom-call(f32[256,128]{1,0:T(8,128)S(1)} %get-tuple-element.9.u_ref, f32[256,128]{1,0:T(8,128)S(1)} %get-tuple-element.10.v_ref, f32[9,16,128]{2,1,0:T(8,128)S(1)} %get-tuple-element.11.dealt), custom_call_target="tpu_custom_call" | custom-call | tf_op jit(solution)/shard_map/pallas_call | solution.py:495

commit v5 on v4

--- a/solution.py
+++ b/solution.py
@@ -49,7 +49,7 @@
 
 def kernel(dims, *refs):
     planes, columns, extent, owners, slabs_x = dims
-    (u_ref, v_ref, u_out, v_out, gathered, loaded, state, edge, packed, got, corner, middle, sums, outgoing,
+    (u_ref, v_ref, u_out, v_out, gathered, loaded, state, edge, packed, folded, got, corner, middle, sums, outgoing,
      load_sem, send_sem, recv_sem, far) = refs
     tiles, pairs, last = extent // LANES, columns // 2, owners - 1
     half = extent // 2
@@ -115,6 +115,10 @@
             tips = pltpu.roll(tips, 4 * at, 1) if at else tips
             pack = jnp.where(group == at, tips, pack)
     packed[...] = pack
+    fold = planes // 2
+    narrow = lax.broadcasted_iota(jnp.int32, (fold, LANES), 1)
+    near_half = lax.rem(narrow + 2, LANES) < LANES // 2
+    folded[...] = jnp.where(near_half, pack[:fold], pltpu.roll(pack[fold:], LANES // 2, 1))
 
     pl.semaphore_wait(barrier, near_count)
 
@@ -138,8 +142,8 @@
         return state.at[:, first_column : first_column + count, :, slice(*spans[part])]
 
     across = [send(0, 0, packed, got.at[side], across_of[side], gy) for side in range(2)]
-    corners_up = [send(0, 1, packed, corner.at[0, side], across_of[side], along_of[0]) for side in range(2)]
-    corners_down = [send(0, 2, packed, corner.at[1, side], across_of[side], along_of[1]) for side in range(2)]
+    corners_up = [send(0, 1, folded, corner.at[0, side], across_of[side], along_of[0]) for side in range(2)]
+    corners_down = [send(0, 2, folded, corner.at[1, side], across_of[side], along_of[1]) for side in range(2)]
     up, down, wrap = [
         [
             send(sender, receiver + 3 * part, columns_of(source, 2, part), columns_of(target, 2, part), gx, along_of[way])
@@ -172,31 +176,37 @@
         for copy in corners_down:
             copy.start()
 
-    for part in parts:
-
+    def start_columns(part):
         @pl.when(gy < last)
         def _():
             up[part].start()
 
-        @pl.when((gy > 0) & (gy < last))
+        @pl.when(gy > 0)
         def _():
             down[part].start()
 
-        @pl.when(gy == last)
-        def _():
-            copies = [up[part], wrap[part]]
-            copies.insert(0 if part == 0 else 2, down[part])
-            for copy in copies:
-                copy.start()
+    start_columns(0)
+
+    @pl.when(gy == last)
+    def _():
+        for part in parts:
+            up[part].start()
+            wrap[part].start()
 
     row = lax.broadcasted_iota(jnp.int32, (half, extent), 0)
     fine = lax.broadcasted_iota(jnp.int32, (half, extent), 1)
     to_level = jnp.where(fine // 2 == row, 0.25, 0.0).astype(jnp.bfloat16)
 
     wait_got(0, got)
+    for part in parts[1:]:
+        start_columns(part)
 
     def merged(below, above):
-        return jnp.where(lax.rem(lane, 4) < 2, above, below)
+        return jnp.where(lax.rem(lane[: below.shape[0]], 4) < 2, above, below)
+
+    def unfolded(way):
+        tips = merged(corner[way, 0], corner[way, 1])
+        return jnp.concatenate([tips, pltpu.roll(tips, LANES // 2, 1)], axis=0)
 
     def place(c, tips, column):
         for field in range(2):
@@ -245,7 +255,7 @@
 
     def wait_side(way, part):
         if part == 0:
-            wait_got(1 + way, state.at[:, 0:3, :, :LANES])
+            wait_got(1 + way, state.at[:, 0:5, :fold, :LANES])
         else:
             up[part].wait_recv() if way == 0 else down[part].wait_recv()
 
@@ -253,39 +263,31 @@
         width = widths[part]
         wait_side(0, part)
         if part == 0:
-            beyond = merged(corner[0, 0], corner[0, 1])
+            beyond = unfolded(0)
             for step in range(1, 4 if wrapped else 2):
                 place(low - step, beyond, columns - step)
         first(low, width)
         first(low - 1, width, () if wrapped else (low - 2,))
-        pair(0, low, width, own=part == final)
+        pair(0, low, width, own=part == final, slot=1 if wrapped else 0)
 
     def high_side(part):
         width = widths[part]
         wait_side(1, part)
         if part == 0:
-            place(high, merged(corner[1, 0], corner[1, 1]), 0)
+            place(high, unfolded(1), 0)
         first(high - 1, width)
         first(high, width, (high + 1,))
         pair(pairs - 1, high - 2, width, own=part == final)
 
-    def level_of(part, slots):
+    def level_of(part, slot):
         width = widths[part]
         contract = (((1,), (1,)), ((), ()))
         taking = to_level[: width // 2, :width]
-        values = jnp.concatenate(
-            [jnp.concatenate([sums[slot, tile] for tile in range(width // LANES)], axis=1) for slot in range(slots)],
-            axis=0,
-        )
-        upper, lower = split(values)
+        upper, lower = split(jnp.concatenate([sums[slot, tile] for tile in range(width // LANES)], axis=1))
         level = lax.dot_general(taking, upper, contract, preferred_element_type=jnp.float32)
         level += lax.dot_general(taking, lower, contract, preferred_element_type=jnp.float32)
-        size = sums.shape[2]
         for owner in range(*shares[part]):
-            for slot in range(slots):
-                outgoing[slot, owner] = level[
-                    owner * portion : (owner + 1) * portion, slot * size : (slot + 1) * size
-                ]
+            outgoing[slot, owner] = level[owner * portion : (owner + 1) * portion]
 
     def deal(slot, owner):
         target = owners if slot else gy
@@ -312,32 +314,33 @@
             def _():
                 pl.semaphore_wait(far, far_count)
 
-        @pl.when(gy == 0)
-        def _():
-            if part == 0:
+        if part == 0:
+
+            @pl.when(gy == 0)
+            def _():
                 for copy in corners_down + down:
                     copy.start()
+
+        level_of(part, 0)
+        for owner in range(*shares[part]):
+
+            @pl.when(owner != gy)
+            def _():
+                deal(0, owner).start()
+
+    @pl.when(gy == 0)
+    def _():
+        for part in parts:
             low_side(part, True)
-
             wrap[part].wait_recv()
             width = widths[part]
             first(low - 2, width)
             first(low - 3, width, (low - 4,))
             pair(pairs - 1, low - 2, width, own=False, slot=1)
-            level_of(part, 2)
+            level_of(part, 1)
             for owner in range(*shares[part]):
                 if owner:
-                    deal(0, owner).start()
                     deal(1, owner).start()
-
-        @pl.when(gy > 0)
-        def _():
-            level_of(part, 1)
-            for owner in range(*shares[part]):
-
-                @pl.when(owner != gy)
-                def _():
-                    deal(0, owner).start()
 
     gathered[gy] = outgoing[0, gy]
 
@@ -346,10 +349,10 @@
         for part in parts[:-1]:
             wait_side(1, part)
             if part == 0:
-                place(high, merged(corner[1, 0], corner[1, 1]), 0)
+                place(high, unfolded(1), 0)
         wait_side(1, final)
         if final == 0:
-            place(high, merged(corner[1, 0], corner[1, 1]), 0)
+            place(high, unfolded(1), 0)
         first(high - 1, extent)
         first(high, extent, (high + 1,))
         pair(pairs - 1, high - 2)
@@ -364,7 +367,7 @@
     def _():
         wait_got(dealt_recv, gathered.at[:owners])
 
-    wait_sent(0, state.at[:, 0:3, :, :LANES])
+    wait_sent(0, state.at[:, 0:2, :, :LANES])
     wait_sent(1, state.at[:, 0:4])
     wait_sent(3, outgoing.at[0, 1:])
 
@@ -396,6 +399,7 @@
     lane = lax.broadcasted_iota(jnp.int32, (portion, LANES), 1)
     even = lax.broadcasted_iota(jnp.int32, (portion, LANES), 0) % 2 == 0
     blocks = [dealt[owner] for owner in range(owners)]
+    blocks[0] = jnp.where(lane % 4 == 0, dealt[owners], blocks[0])
     blocks[-1] = jnp.where(lane % 4 == 3, dealt[owners], blocks[-1])
     width, rows = rebuilt.shape[1], 2 * portion
     chunks = 4
@@ -475,8 +479,9 @@
             pltpu.VMEM((2, columns + 6, planes, extent), f32),
             pltpu.VMEM((2, columns + 6, planes, LANES), f32),
             pltpu.VMEM((planes, LANES), f32),
+            pltpu.VMEM((planes // 2, LANES), f32),
             pltpu.VMEM((2, planes, LANES), f32),
-            pltpu.VMEM((2, 2, planes, LANES), f32),
+            pltpu.VMEM((2, 2, planes // 2, LANES), f32),
             pltpu.VMEM((2, columns + 6, planes, extent + LANES), f32),
             pltpu.VMEM((2, tiles, values, LANES), f32),
             pltpu.VMEM((2, owners, portion, values), f32),
@@ -511,8 +516,10 @@
         rebuilt = rebuilt.reshape(2, planes, rows, width)
     else:
         level = dealt.reshape(owners + 1, portion, 2, planes, pairs)
-        latest = jnp.concatenate([level[owners - 1, ..., :-1], level[owners, ..., -1:]], axis=-1)
-        level = jnp.concatenate([level[: owners - 1], latest[None]], axis=0)
+        outer = level[owners]
+        lowest = jnp.concatenate([outer[..., :1], level[0, ..., 1:]], axis=-1)
+        highest = jnp.concatenate([level[owners - 1, ..., :-1], outer[..., -1:]], axis=-1)
+        level = jnp.concatenate([lowest[None], level[1 : owners - 1], highest[None]], axis=0)
         level = jnp.transpose(level, (2, 3, 1, 0, 4)).reshape(2, planes, portion // 2, 2, columns * owners // 4, 2)
         coarse = 0.25 * jnp.sum(level, axis=(3, 5), keepdims=True)
         blend = (coarse + 0.5 * (level - coarse)).reshape(2, planes, portion, columns * owners // 2)

time: 16.6 us -> 18.1 us (1.090)
  Pallas kernels: 15.8 us -> 17.4 us
    pallas_call x1, Pallas kernels: 14.5 us -> 16.1 us  [body(): pl.pallas_call(functools.partial(kernel, dims), out_shape=(pltpu.VMEM(fla...]
where the time goes in v5:
time: 18.1 us; the launch traced here: 18 us
  Pallas kernels  17.4 us (96%)
  between operations  0.64 us (4%)
    pallas_call x1, Pallas kernels, body(): pl.pallas_call(functools.partial(kernel, dims), out_shape=(pltpu.VMEM(fla...  16.1 us
    pallas_call x1, Pallas kernels, body(): pl.pallas_call(finish, out_shape=(jax.ShapeDtypeStruct(flat, f32), jax.Sh...  1.27 us

profile of v5, /device:TPU:0, one launch (start us, length us, event | category | flops | bytes accessed | tf_op | source)
XLA Modules:
  0.0 18.0 jit_solution(46893585980028335)
XLA Ops:
  0.6 16.1 %shard_map.49 = (f32[256,128]{1,0:T(8,128)S(1)}, f32[256,128]{1,0:T(8,128)S(1)}, f32[9,16,128]{2,1,0:T(8,128)S(1)}) custom-call(f32[256,128]{1,0:T(8,128)} %bitcast.21, f32[256,128]{1,0:T(8,128)} %bitcast.22), custom_call_target="tpu_custom_call" | custom-call | tf_op jit(solution)/shard_map/pallas_call | solution.py:468
  16.7 1.3 %shard_map.50 = (f32[256,128]{1,0:T(8,128)}, f32[256,128]{1,0:T(8,128)}, f32[1024,64]{1,0:T(8,128)}) custom-call(f32[256,128]{1,0:T(8,128)S(1)} %get-tuple-element.9.u_ref, f32[256,128]{1,0:T(8,128)S(1)} %get-tuple-element.10.v_ref, f32[9,16,128]{2,1,0:T(8,128)S(1)} %get-tuple-element.11.dealt), custom_call_target="tpu_custom_call" | custom-call | tf_op jit(solution)/shard_map/pallas_call | solution.py:500

commit v6 on v5

--- a/solution.py
+++ b/solution.py
@@ -176,30 +176,40 @@
         for copy in corners_down:
             copy.start()
 
-    def start_columns(part):
+    @pl.when(gy < last)
+    def _():
+        up[0].start()
+
+    @pl.when(gy > 0)
+    def _():
+        down[0].start()
+
+    @pl.when((gy > 0) & (gy < last))
+    def _():
+        for part in parts[1:]:
+            down[part].start()
+
+    @pl.when(gy == last)
+    def _():
+        for part in parts:
+            up[part].start()
+            wrap[part].start()
+
+    row = lax.broadcasted_iota(jnp.int32, (half, extent), 0)
+    fine = lax.broadcasted_iota(jnp.int32, (half, extent), 1)
+    to_level = jnp.where(fine // 2 == row, 0.25, 0.0).astype(jnp.bfloat16)
+
+    wait_got(0, got)
+    for part in parts[1:]:
+
         @pl.when(gy < last)
         def _():
             up[part].start()
 
-        @pl.when(gy > 0)
+        @pl.when(gy == last)
         def _():
             down[part].start()
 
-    start_columns(0)
-
-    @pl.when(gy == last)
-    def _():
-        for part in parts:
-            up[part].start()
-            wrap[part].start()
-
-    row = lax.broadcasted_iota(jnp.int32, (half, extent), 0)
-    fine = lax.broadcasted_iota(jnp.int32, (half, extent), 1)
-    to_level = jnp.where(fine // 2 == row, 0.25, 0.0).astype(jnp.bfloat16)
-
-    wait_got(0, got)
-    for part in parts[1:]:
-        start_columns(part)
 
     def merged(below, above):
         return jnp.where(lax.rem(lane[: below.shape[0]], 4) < 2, above, below)

time: 18.1 us -> 16 us (0.88)
  Pallas kernels: 17.4 us -> 15.2 us
    pallas_call x1, Pallas kernels: 16.1 us -> 13.9 us  [body(): pl.pallas_call(functools.partial(kernel, dims), out_shape=(pltpu.VMEM(fla...]
where the time goes in v6:
time: 16 us; the launch traced here: 15.8 us
  Pallas kernels  15.2 us (95%)
  between operations  0.64 us (4%)
    pallas_call x1, Pallas kernels, body(): pl.pallas_call(functools.partial(kernel, dims), out_shape=(pltpu.VMEM(fla...  13.9 us
    pallas_call x1, Pallas kernels, body(): pl.pallas_call(finish, out_shape=(jax.ShapeDtypeStruct(flat, f32), jax.Sh...  1.27 us

profile of v6, /device:TPU:0, one launch (start us, length us, event | category | flops | bytes accessed | tf_op | source)
XLA Modules:
  0.0 15.8 jit_solution(7359991159013445220)
XLA Ops:
  0.6 13.9 %shard_map.49 = (f32[256,128]{1,0:T(8,128)S(1)}, f32[256,128]{1,0:T(8,128)S(1)}, f32[9,16,128]{2,1,0:T(8,128)S(1)}) custom-call(f32[256,128]{1,0:T(8,128)} %bitcast.21, f32[256,128]{1,0:T(8,128)} %bitcast.22), custom_call_target="tpu_custom_call" | custom-call | tf_op jit(solution)/shard_map/pallas_call | solution.py:478
  14.5 1.3 %shard_map.50 = (f32[256,128]{1,0:T(8,128)}, f32[256,128]{1,0:T(8,128)}, f32[1024,64]{1,0:T(8,128)}) custom-call(f32[256,128]{1,0:T(8,128)S(1)} %get-tuple-element.9.u_ref, f32[256,128]{1,0:T(8,128)S(1)} %get-tuple-element.10.v_ref, f32[9,16,128]{2,1,0:T(8,128)S(1)} %get-tuple-element.11.dealt), custom_call_target="tpu_custom_call" | custom-call | tf_op jit(solution)/shard_map/pallas_call | solution.py:510

commit v7 on v6

--- a/solution.py
+++ b/solution.py
@@ -42,7 +42,8 @@
 def spread_of(before, here, after):
     planes, extent = here.shape
     total = pltpu.roll(here, 1, 0) + pltpu.roll(here, planes - 1, 0)
-    total = total + before + after
+    for beside in (before, after):
+        total = total if beside is None else total + beside
     total = total + pltpu.roll(here, 1, 1) + pltpu.roll(here, extent - 1, 1)
     return total - 6.0 * here
 
@@ -95,7 +96,7 @@
         load.start()
     pltpu.make_async_copy(loaded, loaded, load_sem).wait()
 
-    low = 4
+    low = 2
     high = low + columns
     lane = lax.broadcasted_iota(jnp.int32, (planes, LANES), 1)
     group = lax.rem(lane + 2, LANES) // 4
@@ -144,18 +145,14 @@
     across = [send(0, 0, packed, got.at[side], across_of[side], gy) for side in range(2)]
     corners_up = [send(0, 1, folded, corner.at[0, side], across_of[side], along_of[0]) for side in range(2)]
     corners_down = [send(0, 2, folded, corner.at[1, side], across_of[side], along_of[1]) for side in range(2)]
-    up, down, wrap = [
+    up, down = [
         [
-            send(sender, receiver + 3 * part, columns_of(source, 2, part), columns_of(target, 2, part), gx, along_of[way])
+            send(1, receiver + 2 * part, columns_of(source, 2, part), columns_of(target, 2, part), gx, along_of[way])
             for part in parts
         ]
-        for sender, receiver, source, target, way in (
-            (1, 1, high - 2, low - 2, 0),
-            (1, 2, low, high, 1),
-            (2, 3, high - 4, low - 4, 0),
-        )
+        for receiver, source, target, way in ((1, high - 2, low - 2, 0), (2, low, high, 1))
     ]
-    dealt_recv = 1 + 3 * len(widths)
+    dealt_recv = 1 + 2 * len(widths)
 
     @pl.when(gy == last)
     def _():
@@ -193,7 +190,6 @@
     def _():
         for part in parts:
             up[part].start()
-            wrap[part].start()
 
     row = lax.broadcasted_iota(jnp.int32, (half, extent), 0)
     fine = lax.broadcasted_iota(jnp.int32, (half, extent), 1)
@@ -261,6 +257,20 @@
                 rows = pl.ds(field * planes * pairs + k, planes, stride=pairs)
                 sums[slot, tile, rows, :] = both_of[0] + both_of[1]
 
+    def side_of_pair(c, before, after, width, slot):
+        here, near = [], []
+        for field in range(2):
+            here.append(half_way(field, c, width))
+            near.append([None if at is None else half_way(field, at, width) for at in (before, after)])
+        spread = [spread_of(near[field][0], here[field], near[field][1])[:, :width] for field in range(2)]
+        inner = [here[field][:, :width] for field in range(2)]
+        new = react(inner[0], inner[1], spread[0], spread[1])
+        for field, diffusion in enumerate((substrate_diffusion, catalyst_diffusion)):
+            total = new[field] + diffusion * inner[field]
+            for tile in range(width // LANES):
+                rows = pl.ds(field * planes * pairs + pairs - 1, planes, stride=pairs)
+                sums[slot, tile, rows, :] = total[:, tile * LANES : (tile + 1) * LANES]
+
     final = len(widths) - 1
 
     def wait_side(way, part):
@@ -274,7 +284,7 @@
         wait_side(0, part)
         if part == 0:
             beyond = unfolded(0)
-            for step in range(1, 4 if wrapped else 2):
+            for step in range(1, 3 if wrapped else 2):
                 place(low - step, beyond, columns - step)
         first(low, width)
         first(low - 1, width, () if wrapped else (low - 2,))
@@ -301,13 +311,17 @@
 
     def deal(slot, owner):
         target = owners if slot else gy
-        return send(3 + slot, dealt_recv, outgoing.at[slot, owner], gathered.at[target], gx, owner)
+        return send(2 + slot, dealt_recv, outgoing.at[slot, owner], gathered.at[target], gx, owner)
 
     for c in range(low + 1, high - 1):
         first(c, extent)
     for k in range(1, pairs - 1):
         pair(k, low + 2 * k)
 
+    @pl.when(gy == last)
+    def _():
+        side_of_pair(high - 2, high - 3, None, extent, 0)
+
     for part in parts:
 
         @pl.when(gy > 0)
@@ -342,11 +356,7 @@
     def _():
         for part in parts:
             low_side(part, True)
-            wrap[part].wait_recv()
-            width = widths[part]
-            first(low - 2, width)
-            first(low - 3, width, (low - 4,))
-            pair(pairs - 1, low - 2, width, own=False, slot=1)
+            side_of_pair(low - 1, None, low, widths[part], 1)
             level_of(part, 1)
             for owner in range(*shares[part]):
                 if owner:
@@ -371,7 +381,7 @@
     def _():
         gathered[owners] = outgoing[1, 0]
         wait_got(dealt_recv, gathered.at[1:owners])
-        wait_sent(4, outgoing.at[1, 1:])
+        wait_sent(3, outgoing.at[1, 1:])
 
     @pl.when(gy > 0)
     def _():
@@ -379,11 +389,7 @@
 
     wait_sent(0, state.at[:, 0:2, :, :LANES])
     wait_sent(1, state.at[:, 0:4])
-    wait_sent(3, outgoing.at[0, 1:])
-
-    @pl.when(gy == last)
-    def _():
-        wait_sent(2, state.at[:, 0:2])
+    wait_sent(2, outgoing.at[0, 1:])
 
 
 def finish(u_ref, v_ref, dealt, u_out, v_out, rebuilt_out, doubled, paired, rebuilt, sems):
@@ -410,7 +416,7 @@
     even = lax.broadcasted_iota(jnp.int32, (portion, LANES), 0) % 2 == 0
     blocks = [dealt[owner] for owner in range(owners)]
     blocks[0] = jnp.where(lane % 4 == 0, dealt[owners], blocks[0])
-    blocks[-1] = jnp.where(lane % 4 == 3, dealt[owners], blocks[-1])
+    blocks[-1] = jnp.where(lane % 4 == 3, blocks[-1] + dealt[owners], blocks[-1])
     width, rows = rebuilt.shape[1], 2 * portion
     chunks = 4
     share = 8 // chunks
@@ -486,18 +492,18 @@
         out_specs=(vmem,) * 3,
         scratch_shapes=[
             pltpu.VMEM((2,) + flat, f32),
-            pltpu.VMEM((2, columns + 6, planes, extent), f32),
-            pltpu.VMEM((2, columns + 6, planes, LANES), f32),
+            pltpu.VMEM((2, columns + 4, planes, extent), f32),
+            pltpu.VMEM((2, columns + 4, planes, LANES), f32),
             pltpu.VMEM((planes, LANES), f32),
             pltpu.VMEM((planes // 2, LANES), f32),
             pltpu.VMEM((2, planes, LANES), f32),
             pltpu.VMEM((2, 2, planes // 2, LANES), f32),
-            pltpu.VMEM((2, columns + 6, planes, extent + LANES), f32),
+            pltpu.VMEM((2, columns + 4, planes, extent + LANES), f32),
             pltpu.VMEM((2, tiles, values, LANES), f32),
             pltpu.VMEM((2, owners, portion, values), f32),
             pltpu.SemaphoreType.DMA,
-            pltpu.SemaphoreType.DMA((5,)),
-            pltpu.SemaphoreType.DMA((8 if tiles > 1 else 5,)),
+            pltpu.SemaphoreType.DMA((4,)),
+            pltpu.SemaphoreType.DMA((6 if tiles > 1 else 4,)),
             pltpu.SemaphoreType.REGULAR,
         ],
         compiler_params=pltpu.CompilerParams(collective_id=0, has_side_effects=True),
@@ -528,7 +534,8 @@
         level = dealt.reshape(owners + 1, portion, 2, planes, pairs)
         outer = level[owners]
         lowest = jnp.concatenate([outer[..., :1], level[0, ..., 1:]], axis=-1)
-        highest = jnp.concatenate([level[owners - 1, ..., :-1], outer[..., -1:]], axis=-1)
+        highest = level[owners - 1]
+        highest = jnp.concatenate([highest[..., :-1], highest[..., -1:] + outer[..., -1:]], axis=-1)
         level = jnp.concatenate([lowest[None], level[1 : owners - 1], highest[None]], axis=0)
         level = jnp.transpose(level, (2, 3, 1, 0, 4)).reshape(2, planes, portion // 2, 2, columns * owners // 4, 2)
         coarse = 0.25 * jnp.sum(level, axis=(3, 5), keepdims=True)

time: 16 us -> 15.4 us (0.963)
  Pallas kernels: 15.2 us -> 14.6 us
    pallas_call x1, Pallas kernels: 13.9 us -> 13.4 us  [body(): pl.pallas_call(functools.partial(kernel, dims), out_shape=(pltpu.VMEM(fla...]
where the time goes in v7:
time: 15.4 us; the launch traced here: 15.3 us
  Pallas kernels  14.6 us (95%)
  between operations  0.64 us (4%)
    pallas_call x1, Pallas kernels, body(): pl.pallas_call(functools.partial(kernel, dims), out_shape=(pltpu.VMEM(fla...  13.4 us
    pallas_call x1, Pallas kernels, body(): pl.pallas_call(finish, out_shape=(jax.ShapeDtypeStruct(flat, f32), jax.Sh...  1.27 us

profile of v7, /device:TPU:0, one launch (start us, length us, event | category | flops | bytes accessed | tf_op | source)
XLA Modules:
  0.0 15.3 jit_solution(4489993809694228087)
XLA Ops:
  0.6 13.4 %shard_map.49 = (f32[256,128]{1,0:T(8,128)S(1)}, f32[256,128]{1,0:T(8,128)S(1)}, f32[9,16,128]{2,1,0:T(8,128)S(1)}) custom-call(f32[256,128]{1,0:T(8,128)} %bitcast.21, f32[256,128]{1,0:T(8,128)} %bitcast.22), custom_call_target="tpu_custom_call" | custom-call | tf_op jit(solution)/shard_map/pallas_call | solution.py:484
  14.0 1.3 %shard_map.50 = (f32[256,128]{1,0:T(8,128)}, f32[256,128]{1,0:T(8,128)}, f32[1024,64]{1,0:T(8,128)}) custom-call(f32[256,128]{1,0:T(8,128)S(1)} %get-tuple-element.9.u_ref, f32[256,128]{1,0:T(8,128)S(1)} %get-tuple-element.10.v_ref, f32[9,16,128]{2,1,0:T(8,128)S(1)} %get-tuple-element.11.dealt), custom_call_target="tpu_custom_call" | custom-call | tf_op jit(solution)/shard_map/pallas_call | solution.py:516

commit v8 on v7

--- a/solution.py
+++ b/solution.py
@@ -48,9 +48,23 @@
     return total - 6.0 * here
 
 
+def spreading_of():
+    wide_in = lax.broadcasted_iota(jnp.int32, (LANES, 4 * LANES), 0)
+    wide_out = lax.broadcasted_iota(jnp.int32, (LANES, 4 * LANES), 1)
+    column_of = wide_in // 16 * 4 + wide_in % 4
+    plane = wide_in // 4 % 4 == wide_out // LANES
+    return jnp.concatenate(
+        [
+            jnp.where(plane & (column_of == wide_out % LANES // 2), 0.5, 0.0),
+            jnp.where(plane & (column_of // 2 == wide_out % LANES // 4), 0.125, 0.0),
+        ],
+        axis=0,
+    ).astype(jnp.bfloat16)
+
+
 def kernel(dims, *refs):
     planes, columns, extent, owners, slabs_x = dims
-    (u_ref, v_ref, u_out, v_out, gathered, loaded, state, edge, packed, folded, got, corner, middle, sums, outgoing,
+    (u_ref, v_ref, u_out, v_out, gathered, spreading, loaded, state, edge, packed, folded, got, corner, middle, sums, outgoing,
      load_sem, send_sem, recv_sem, far) = refs
     tiles, pairs, last = extent // LANES, columns // 2, owners - 1
     half = extent // 2
@@ -195,6 +209,8 @@
     fine = lax.broadcasted_iota(jnp.int32, (half, extent), 1)
     to_level = jnp.where(fine // 2 == row, 0.25, 0.0).astype(jnp.bfloat16)
 
+    spreading[...] = spreading_of()
+
     wait_got(0, got)
     for part in parts[1:]:
 
@@ -304,8 +320,12 @@
         contract = (((1,), (1,)), ((), ()))
         taking = to_level[: width // 2, :width]
         upper, lower = split(jnp.concatenate([sums[slot, tile] for tile in range(width // LANES)], axis=1))
-        level = lax.dot_general(taking, upper, contract, preferred_element_type=jnp.float32)
-        level += lax.dot_general(taking, lower, contract, preferred_element_type=jnp.float32)
+        level = lax.dot_general(
+            jnp.concatenate([taking, taking], axis=1),
+            jnp.concatenate([upper, lower], axis=1),
+            contract,
+            preferred_element_type=jnp.float32,
+        )
         for owner in range(*shares[part]):
             outgoing[slot, owner] = level[owner * portion : (owner + 1) * portion]
 
@@ -392,7 +412,7 @@
     wait_sent(2, outgoing.at[0, 1:])
 
 
-def finish(u_ref, v_ref, dealt, u_out, v_out, rebuilt_out, doubled, paired, rebuilt, sems):
+def finish(u_ref, v_ref, dealt, spreading, u_out, v_out, rebuilt_out, doubled, paired, rebuilt, sems):
     copies = [
         pltpu.make_async_copy(u_ref, u_out, sems.at[0]),
         pltpu.make_async_copy(v_ref, v_out, sems.at[1]),
@@ -401,17 +421,6 @@
         copy.start()
 
     owners, portion = dealt.shape[0] - 1, dealt.shape[1]
-    wide_in = lax.broadcasted_iota(jnp.int32, (LANES, 4 * LANES), 0)
-    wide_out = lax.broadcasted_iota(jnp.int32, (LANES, 4 * LANES), 1)
-    column_of = wide_in // 16 * 4 + wide_in % 4
-    plane = wide_in // 4 % 4 == wide_out // LANES
-    spreading = jnp.concatenate(
-        [
-            jnp.where(plane & (column_of == wide_out % LANES // 2), 0.5, 0.0),
-            jnp.where(plane & (column_of // 2 == wide_out % LANES // 4), 0.125, 0.0),
-        ],
-        axis=0,
-    ).astype(jnp.bfloat16)
     lane = lax.broadcasted_iota(jnp.int32, (portion, LANES), 1)
     even = lax.broadcasted_iota(jnp.int32, (portion, LANES), 0) % 2 == 0
     blocks = [dealt[owner] for owner in range(owners)]
@@ -434,8 +443,11 @@
                 paired[pl.ds(h * rows + twin, portion, stride=2), :] = total
         span = slice(chunk * share * rows, (chunk + 1) * share * rows)
         high, low = split(jnp.concatenate([doubled[span, :], paired[span, :]], axis=1))
-        whole = jnp.dot(high, spreading, preferred_element_type=jnp.float32)
-        whole += jnp.dot(low, spreading, preferred_element_type=jnp.float32)
+        whole = jnp.dot(
+            jnp.concatenate([high, low], axis=1),
+            jnp.concatenate([spreading[...], spreading[...]], axis=0),
+            preferred_element_type=jnp.float32,
+        )
         for h in range(share):
             for z in range(4):
                 base = ((chunk * share + h) * 4 + z) * rows
@@ -481,15 +493,16 @@
     flat = (planes * tiles * columns, LANES)
     vmem = pl.BlockSpec(memory_space=pltpu.VMEM)
     anywhere = pl.BlockSpec(memory_space=pl.ANY)
-    u, v, dealt = pl.pallas_call(
+    u, v, dealt, spreading = pl.pallas_call(
         functools.partial(kernel, dims),
         out_shape=(
             pltpu.VMEM(flat, f32),
             pltpu.VMEM(flat, f32),
             pltpu.VMEM((owners + 1, portion, values), f32),
+            pltpu.VMEM((2 * LANES, 4 * LANES), jnp.bfloat16),
         ),
         in_specs=[anywhere] * 2,
-        out_specs=(vmem,) * 3,
+        out_specs=(vmem,) * 4,
         scratch_shapes=[
             pltpu.VMEM((2,) + flat, f32),
             pltpu.VMEM((2, columns + 4, planes, extent), f32),
@@ -510,8 +523,8 @@
     )(tiled(substrate), tiled(catalyst))
     rows, width = 2 * portion, columns * owners
     if fused:
-        u, v, dealt = (
-            pltpu.with_memory_space_constraint(x, pltpu.VMEM) for x in (u, v, dealt)
+        u, v, dealt, spreading = (
+            pltpu.with_memory_space_constraint(x, pltpu.VMEM) for x in (u, v, dealt, spreading)
         )
         u, v, rebuilt = pl.pallas_call(
             finish,
@@ -520,7 +533,7 @@
                 jax.ShapeDtypeStruct(flat, f32),
                 jax.ShapeDtypeStruct((2 * planes * rows, width), f32),
             ),
-            in_specs=[vmem] * 3,
+            in_specs=[vmem] * 4,
             out_specs=(anywhere,) * 3,
             scratch_shapes=[
                 pltpu.VMEM((8 * rows, LANES), f32),
@@ -528,7 +541,7 @@
                 pltpu.VMEM((2 * planes * rows, width), f32),
                 pltpu.SemaphoreType.DMA((3,)),
             ],
-        )(u, v, dealt)
+        )(u, v, dealt, spreading)
         rebuilt = rebuilt.reshape(2, planes, rows, width)
     else:
         level = dealt.reshape(owners + 1, portion, 2, planes, pairs)

time: 15.4 us -> 15.4 us (level)
  no operation moved by 1% of the time
where the time goes in v8:
time: 15.4 us; the launch traced here: 15.2 us
  Pallas kernels  14.6 us (95%)
  between operations  0.64 us (4%)
    pallas_call x1, Pallas kernels, body(): pl.pallas_call(functools.partial(kernel, dims), out_shape=(pltpu.VMEM(fla...  13.3 us
    pallas_call x1, Pallas kernels, body(): pl.pallas_call(finish, out_shape=(jax.ShapeDtypeStruct(flat, f32), jax.Sh...  1.24 us

profile of v8, /device:TPU:0, one launch (start us, length us, event | category | flops | bytes accessed | tf_op | source)
XLA Modules:
  0.0 15.2 jit_solution(4062911419619820525)
XLA Ops:
  0.6 13.3 %shard_map.49 = (f32[256,128]{1,0:T(8,128)S(1)}, f32[256,128]{1,0:T(8,128)S(1)}, f32[9,16,128]{2,1,0:T(8,128)S(1)}, bf16[256,512]{1,0:T(8,128)(2,1)S(1)}) custom-call(f32[256,128]{1,0:T(8,128)} %bitcast.21, f32[256,128]{1,0:T(8,128)} %bitcast.22), custom_call_target="tpu_custom_call" | custom-call | tf_op jit(solution)/shard_map/pallas_call | solution.py:496
  14.0 1.2 %shard_map.50 = (f32[256,128]{1,0:T(8,128)}, f32[256,128]{1,0:T(8,128)}, f32[1024,64]{1,0:T(8,128)}) custom-call(f32[256,128]{1,0:T(8,128)S(1)} %get-tuple-element.10.u_ref, f32[256,128]{1,0:T(8,128)S(1)} %get-tuple-element.11.v_ref, f32[9,16,128]{2,1,0:T(8,128)S(1)} %get-tuple-element.12.dealt, bf16[256,512]{1,0:T(8,128)(2,1)S(1)} %get-tuple-element.13.spreading), custom_call_target="tpu_custom_call" | custom-call | tf_op jit(solution)/shard_map/pallas_call | solution.py:529

commit v9 on v8

--- a/solution.py
+++ b/solution.py
@@ -112,28 +112,19 @@
 
     low = 2
     high = low + columns
-    lane = lax.broadcasted_iota(jnp.int32, (planes, LANES), 1)
-    group = lax.rem(lane + 2, LANES) // 4
-    pack = jnp.zeros((planes, LANES), jnp.float32)
-    for field in range(2):
-        for column in range(columns):
-            slab = jnp.concatenate(
+    def lay_out(column):
+        for field in range(2):
+            state[field, low + column] = jnp.concatenate(
                 [
                     loaded[field, pl.ds(tile * columns + column, planes, stride=tiles * columns), :]
                     for tile in range(tiles)
                 ],
                 axis=1,
             )
-            state[field, low + column] = slab
-            at = field * columns + column
-            tips = jnp.where(lane < LANES // 2, slab[:, :LANES], slab[:, extent - LANES :])
-            tips = pltpu.roll(tips, 4 * at, 1) if at else tips
-            pack = jnp.where(group == at, tips, pack)
-    packed[...] = pack
-    fold = planes // 2
-    narrow = lax.broadcasted_iota(jnp.int32, (fold, LANES), 1)
-    near_half = lax.rem(narrow + 2, LANES) < LANES // 2
-    folded[...] = jnp.where(near_half, pack[:fold], pltpu.roll(pack[fold:], LANES // 2, 1))
+
+    outer_columns = (0, 1, columns - 2, columns - 1)
+    for column in outer_columns:
+        lay_out(column)
 
     pl.semaphore_wait(barrier, near_count)
 
@@ -179,6 +170,34 @@
         def _():
             greet(far, gx, peer)
 
+    up[0].start()
+
+    @pl.when(gy > 0)
+    def _():
+        down[0].start()
+
+    for column in range(columns):
+        if column not in outer_columns:
+            lay_out(column)
+    lane = lax.broadcasted_iota(jnp.int32, (planes, LANES), 1)
+    group = lax.rem(lane + 2, LANES) // 4
+    pack = jnp.zeros((planes, LANES), jnp.float32)
+    for field in range(2):
+        for column in range(columns):
+            at = field * columns + column
+            tips = jnp.where(
+                lane < LANES // 2,
+                state[field, low + column, :, :LANES],
+                state[field, low + column, :, extent - LANES :],
+            )
+            tips = pltpu.roll(tips, 4 * at, 1) if at else tips
+            pack = jnp.where(group == at, tips, pack)
+    packed[...] = pack
+    fold = planes // 2
+    narrow = lax.broadcasted_iota(jnp.int32, (fold, LANES), 1)
+    near_half = lax.rem(narrow + 2, LANES) < LANES // 2
+    folded[...] = jnp.where(near_half, pack[:fold], pltpu.roll(pack[fold:], LANES // 2, 1))
+
     for copy in across + corners_up:
         copy.start()
 
@@ -187,14 +206,6 @@
         for copy in corners_down:
             copy.start()
 
-    @pl.when(gy < last)
-    def _():
-        up[0].start()
-
-    @pl.when(gy > 0)
-    def _():
-        down[0].start()
-
     @pl.when((gy > 0) & (gy < last))
     def _():
         for part in parts[1:]:
@@ -202,7 +213,7 @@
 
     @pl.when(gy == last)
     def _():
-        for part in parts:
+        for part in parts[1:]:
             up[part].start()
 
     row = lax.broadcasted_iota(jnp.int32, (half, extent), 0)
@@ -295,25 +306,28 @@
         else:
             up[part].wait_recv() if way == 0 else down[part].wait_recv()
 
-    def low_side(part, wrapped):
+    def sides(part, below=True, above=True, wrapped=False):
         width = widths[part]
-        wait_side(0, part)
-        if part == 0:
-            beyond = unfolded(0)
-            for step in range(1, 3 if wrapped else 2):
-                place(low - step, beyond, columns - step)
-        first(low, width)
-        first(low - 1, width, () if wrapped else (low - 2,))
-        pair(0, low, width, own=part == final, slot=1 if wrapped else 0)
-
-    def high_side(part):
-        width = widths[part]
-        wait_side(1, part)
-        if part == 0:
-            place(high, unfolded(1), 0)
-        first(high - 1, width)
-        first(high, width, (high + 1,))
-        pair(pairs - 1, high - 2, width, own=part == final)
+        if below:
+            wait_side(0, part)
+            if part == 0:
+                beyond = unfolded(0)
+                for step in range(1, 3 if wrapped else 2):
+                    place(low - step, beyond, columns - step)
+        if above:
+            wait_side(1, part)
+            if part == 0:
+                place(high, unfolded(1), 0)
+        if below:
+            first(low, width)
+            first(low - 1, width, () if wrapped else (low - 2,))
+        if above:
+            first(high - 1, width)
+            first(high, width, (high + 1,))
+        if below:
+            pair(0, low, width, own=part == final, slot=1 if wrapped else 0)
+        if above:
+            pair(pairs - 1, high - 2, width, own=part == final)
 
     def level_of(part, slot):
         width = widths[part]
@@ -344,13 +358,17 @@
 
     for part in parts:
 
-        @pl.when(gy > 0)
-        def _():
-            low_side(part, False)
-
-        @pl.when(gy < last)
-        def _():
-            high_side(part)
+        @pl.when((gy > 0) & (gy < last))
+        def _():
+            sides(part)
+
+        @pl.when(gy == last)
+        def _():
+            sides(part, above=False)
+
+        @pl.when(gy == 0)
+        def _():
+            sides(part, below=False)
 
         if part == 0:
 
@@ -375,7 +393,7 @@
     @pl.when(gy == 0)
     def _():
         for part in parts:
-            low_side(part, True)
+            sides(part, above=False, wrapped=True)
             side_of_pair(low - 1, None, low, widths[part], 1)
             level_of(part, 1)
             for owner in range(*shares[part]):

time: 15.4 us -> 15.4 us (level)
  no operation moved by 1% of the time
where the time goes in v9:
time: 15.4 us; the launch traced here: 15.2 us
  Pallas kernels  14.6 us (95%)
  between operations  0.64 us (4%)
    pallas_call x1, Pallas kernels, body(): pl.pallas_call(functools.partial(kernel, dims), out_shape=(pltpu.VMEM(fla...  13.4 us
    pallas_call x1, Pallas kernels, body(): pl.pallas_call(finish, out_shape=(jax.ShapeDtypeStruct(flat, f32), jax.Sh...  1.24 us

profile of v9, /device:TPU:0, one launch (start us, length us, event | category | flops | bytes accessed | tf_op | source)
XLA Modules:
  0.0 15.2 jit_solution(4092193311550645812)
XLA Ops:
  0.6 13.4 %shard_map.49 = (f32[256,128]{1,0:T(8,128)S(1)}, f32[256,128]{1,0:T(8,128)S(1)}, f32[9,16,128]{2,1,0:T(8,128)S(1)}, bf16[256,512]{1,0:T(8,128)(2,1)S(1)}) custom-call(f32[256,128]{1,0:T(8,128)} %bitcast.21, f32[256,128]{1,0:T(8,128)} %bitcast.22), custom_call_target="tpu_custom_call" | custom-call | tf_op jit(solution)/shard_map/pallas_call | solution.py:514
  14.0 1.2 %shard_map.50 = (f32[256,128]{1,0:T(8,128)}, f32[256,128]{1,0:T(8,128)}, f32[1024,64]{1,0:T(8,128)}) custom-call(f32[256,128]{1,0:T(8,128)S(1)} %get-tuple-element.10.u_ref, f32[256,128]{1,0:T(8,128)S(1)} %get-tuple-element.11.v_ref, f32[9,16,128]{2,1,0:T(8,128)S(1)} %get-tuple-element.12.dealt, bf16[256,512]{1,0:T(8,128)(2,1)S(1)} %get-tuple-element.13.spreading), custom_call_target="tpu_custom_call" | custom-call | tf_op jit(solution)/shard_map/pallas_call | solution.py:547

commit v10 on v9

--- a/solution.py
+++ b/solution.py
@@ -445,38 +445,36 @@
     blocks[0] = jnp.where(lane % 4 == 0, dealt[owners], blocks[0])
     blocks[-1] = jnp.where(lane % 4 == 3, blocks[-1] + dealt[owners], blocks[-1])
     width, rows = rebuilt.shape[1], 2 * portion
-    chunks = 4
-    share = 8 // chunks
-    for chunk in range(chunks):
-        for h in range(chunk * share, (chunk + 1) * share):
-            part = jnp.zeros((portion, LANES), jnp.float32)
-            for owner in range(8):
-                shift = (16 * (owner - h)) % LANES
-                moved = pltpu.roll(blocks[owner], shift, 1) if shift else blocks[owner]
-                part = jnp.where(lane // 16 == owner, moved, part)
-            other = jnp.where(even, pltpu.roll(part, portion - 1, 0), pltpu.roll(part, 1, 0))
-            total = part + other
-            for twin in range(2):
-                doubled[pl.ds(h * rows + twin, portion, stride=2), :] = part
-                paired[pl.ds(h * rows + twin, portion, stride=2), :] = total
-        span = slice(chunk * share * rows, (chunk + 1) * share * rows)
-        high, low = split(jnp.concatenate([doubled[span, :], paired[span, :]], axis=1))
-        whole = jnp.dot(
-            jnp.concatenate([high, low], axis=1),
-            jnp.concatenate([spreading[...], spreading[...]], axis=0),
-            preferred_element_type=jnp.float32,
-        )
-        for h in range(share):
+    groups, quarters = 8, 4
+    for h in range(groups):
+        part = jnp.zeros((portion, LANES), jnp.float32)
+        for owner in range(8):
+            shift = (16 * (owner - h)) % LANES
+            moved = pltpu.roll(blocks[owner], shift, 1) if shift else blocks[owner]
+            part = jnp.where(lane // 16 == owner, moved, part)
+        other = jnp.where(even, pltpu.roll(part, portion - 1, 0), pltpu.roll(part, 1, 0))
+        total = part + other
+        for twin in range(2):
+            doubled[pl.ds(h * rows + twin, portion, stride=2), :] = part
+            paired[pl.ds(h * rows + twin, portion, stride=2), :] = total
+    high, low = split(jnp.concatenate([doubled[...], paired[...]], axis=1))
+    whole = jnp.dot(
+        jnp.concatenate([high, low], axis=1),
+        jnp.concatenate([spreading[...], spreading[...]], axis=0),
+        preferred_element_type=jnp.float32,
+    )
+    size = groups // quarters * 4 * rows
+    for quarter in range(quarters):
+        for h in range(quarter * groups // quarters, (quarter + 1) * groups // quarters):
             for z in range(4):
-                base = ((chunk * share + h) * 4 + z) * rows
+                base = (h * 4 + z) * rows
                 rebuilt[base : base + rows, :] = whole[
                     h * rows : (h + 1) * rows, z * LANES : z * LANES + width
                 ]
-        size = share * 4 * rows
         copies.append(
             pltpu.make_async_copy(
-                rebuilt.at[chunk * size : (chunk + 1) * size],
-                rebuilt_out.at[chunk * size : (chunk + 1) * size],
+                rebuilt.at[quarter * size : (quarter + 1) * size],
+                rebuilt_out.at[quarter * size : (quarter + 1) * size],
                 sems.at[2],
             )
         )

time: 15.4 us -> 15.3 us (level)
  no operation moved by 1% of the time
where the time goes in v10:
time: 15.3 us; the launch traced here: 15.2 us
  Pallas kernels  14.6 us (95%)
  between operations  0.64 us (4%)
    pallas_call x1, Pallas kernels, body(): pl.pallas_call(functools.partial(kernel, dims), out_shape=(pltpu.VMEM(fla...  13.4 us
    pallas_call x1, Pallas kernels, body(): pl.pallas_call(finish, out_shape=(jax.ShapeDtypeStruct(flat, f32), jax.Sh...  1.19 us

profile of v10, /device:TPU:0, one launch (start us, length us, event | category | flops | bytes accessed | tf_op | source)
XLA Modules:
  0.0 15.2 jit_solution(10062640951063862317)
XLA Ops:
  0.6 13.4 %shard_map.49 = (f32[256,128]{1,0:T(8,128)S(1)}, f32[256,128]{1,0:T(8,128)S(1)}, f32[9,16,128]{2,1,0:T(8,128)S(1)}, bf16[256,512]{1,0:T(8,128)(2,1)S(1)}) custom-call(f32[256,128]{1,0:T(8,128)} %bitcast.21, f32[256,128]{1,0:T(8,128)} %bitcast.22), custom_call_target="tpu_custom_call" | custom-call | tf_op jit(solution)/shard_map/pallas_call | solution.py:512
  14.0 1.2 %shard_map.50 = (f32[256,128]{1,0:T(8,128)}, f32[256,128]{1,0:T(8,128)}, f32[1024,64]{1,0:T(8,128)}) custom-call(f32[256,128]{1,0:T(8,128)S(1)} %get-tuple-element.10.u_ref, f32[256,128]{1,0:T(8,128)S(1)} %get-tuple-element.11.v_ref, f32[9,16,128]{2,1,0:T(8,128)S(1)} %get-tuple-element.12.dealt, bf16[256,512]{1,0:T(8,128)(2,1)S(1)} %get-tuple-element.13.spreading), custom_call_target="tpu_custom_call" | custom-call | tf_op jit(solution)/shard_map/pallas_call | solution.py:545

commit v11 on v10

--- a/solution.py
+++ b/solution.py
@@ -152,7 +152,7 @@
     corners_down = [send(0, 2, folded, corner.at[1, side], across_of[side], along_of[1]) for side in range(2)]
     up, down = [
         [
-            send(1, receiver + 2 * part, columns_of(source, 2, part), columns_of(target, 2, part), gx, along_of[way])
+            send(0, receiver + 2 * part, columns_of(source, 2, part), columns_of(target, 2, part), gx, along_of[way])
             for part in parts
         ]
         for receiver, source, target, way in ((1, high - 2, low - 2, 0), (2, low, high, 1))
@@ -345,7 +345,7 @@
 
     def deal(slot, owner):
         target = owners if slot else gy
-        return send(2 + slot, dealt_recv, outgoing.at[slot, owner], gathered.at[target], gx, owner)
+        return send(1 + slot, dealt_recv, outgoing.at[slot, owner], gathered.at[target], gx, owner)
 
     for c in range(low + 1, high - 1):
         first(c, extent)
@@ -419,15 +419,14 @@
     def _():
         gathered[owners] = outgoing[1, 0]
         wait_got(dealt_recv, gathered.at[1:owners])
-        wait_sent(3, outgoing.at[1, 1:])
+        wait_sent(2, outgoing.at[1, 1:])
 
     @pl.when(gy > 0)
     def _():
         wait_got(dealt_recv, gathered.at[:owners])
 
-    wait_sent(0, state.at[:, 0:2, :, :LANES])
-    wait_sent(1, state.at[:, 0:4])
-    wait_sent(2, outgoing.at[0, 1:])
+    wait_sent(0, state.at[:, 0 : 2 + 4 * tiles, :, :LANES])
+    wait_sent(1, outgoing.at[0, 1:])
 
 
 def finish(u_ref, v_ref, dealt, spreading, u_out, v_out, rebuilt_out, doubled, paired, rebuilt, sems):
@@ -531,7 +530,7 @@
             pltpu.VMEM((2, tiles, values, LANES), f32),
             pltpu.VMEM((2, owners, portion, values), f32),
             pltpu.SemaphoreType.DMA,
-            pltpu.SemaphoreType.DMA((4,)),
+            pltpu.SemaphoreType.DMA((3,)),
             pltpu.SemaphoreType.DMA((6 if tiles > 1 else 4,)),
             pltpu.SemaphoreType.REGULAR,
         ],

time: 15.3 us -> 15.3 us (level)
  no operation moved by 1% of the time
where the time goes in v11:
time: 15.3 us; the launch traced here: 15.2 us
  Pallas kernels  14.6 us (95%)
  between operations  0.64 us (4%)
    pallas_call x1, Pallas kernels, body(): pl.pallas_call(functools.partial(kernel, dims), out_shape=(pltpu.VMEM(fla...  13.4 us
    pallas_call x1, Pallas kernels, body(): pl.pallas_call(finish, out_shape=(jax.ShapeDtypeStruct(flat, f32), jax.Sh...  1.19 us

profile of v11, /device:TPU:0, one launch (start us, length us, event | category | flops | bytes accessed | tf_op | source)
XLA Modules:
  0.0 15.2 jit_solution(17846879037764868779)
XLA Ops:
  0.6 13.4 %shard_map.49 = (f32[256,128]{1,0:T(8,128)S(1)}, f32[256,128]{1,0:T(8,128)S(1)}, f32[9,16,128]{2,1,0:T(8,128)S(1)}, bf16[256,512]{1,0:T(8,128)(2,1)S(1)}) custom-call(f32[256,128]{1,0:T(8,128)} %bitcast.21, f32[256,128]{1,0:T(8,128)} %bitcast.22), custom_call_target="tpu_custom_call" | custom-call | tf_op jit(solution)/shard_map/pallas_call | solution.py:511
  14.0 1.2 %shard_map.50 = (f32[256,128]{1,0:T(8,128)}, f32[256,128]{1,0:T(8,128)}, f32[1024,64]{1,0:T(8,128)}) custom-call(f32[256,128]{1,0:T(8,128)S(1)} %get-tuple-element.10.u_ref, f32[256,128]{1,0:T(8,128)S(1)} %get-tuple-element.11.v_ref, f32[9,16,128]{2,1,0:T(8,128)S(1)} %get-tuple-element.12.dealt, bf16[256,512]{1,0:T(8,128)(2,1)S(1)} %get-tuple-element.13.spreading), custom_call_target="tpu_custom_call" | custom-call | tf_op jit(solution)/shard_map/pallas_call | solution.py:544
